TPU v7x, 32 devices: a whole 2x2x4 slice. The times are simulated.
32 devices in a mesh: dom: 4 (over z), col: 4 (over y, core), rep: 2 (over x).
Axes of the slice: x: 2, y: 2, z: 4, core: 2. Of those that a mesh axis runs over, the one named last changes fastest.
Arguments:
- features: bfloat16 [2, 4096, 100], P('rep', 'dom'), may hold values from -6 to 6
- w_in: bfloat16 [100, 256], P(None, 'col'), may hold values from -0.625 to 0.625
- w_hidden: bfloat16 [256, 256], P('col'), may hold values from -0.375 to 0.375
- blocks: bfloat16 [2, 4, 8, 512, 512], P('rep', 'dom'), may hold values from -0.125 to 0.125
- block_list: int32 [2, 4, 8, 3], P('rep', 'dom'), may hold values from 0 to 3, as said below
- block_count: int32 [2, 4], P('rep', 'dom'), may hold values from 1 to 8, as said below
- cotangent: bfloat16 [2, 4096, 256], P('rep', 'dom', 'col'), may hold values from -6 to 6
Outputs:
- out_hidden: bfloat16 [2, 4096, 256], P('rep', 'dom', 'col')
- grad_hidden: float32 [256, 256], P('col', ('dom', 'rep'))
Inputs may be any that keep to these rules, and one draw needn't show every extreme that they name: `block_list`: each slot holds a row cluster below 2, a partner partition below 4 and a partner cluster below 2; the same cluster pair may stand in several slots, and then their blocks add. `block_count`: in every batch some partition uses all 8 slots.
All inputs are finite; a program needn't handle non-finite values.
Results may differ from a plain program's by a relative error of at most 0.0065.
Values may be sent and summed in bfloat16 or wider, within the bound.
No kernel may reach another device: no remote copies, remote signals or barrier semaphores. Data moves between devices by JAX's collectives and lax.ppermute only.
A program may use at most 64 MiB of HBM per device.

v0:
```python
import jax
import jax.numpy as jnp
from jax import lax
from jax.sharding import PartitionSpec as P


def body(features, w_in, w_hidden, blocks, block_list, block_count, cotangent):
    rows = features.shape[1]
    slots = blocks.shape[2]
    clus = blocks.shape[3]
    width = w_in.shape[1]
    local_blocks = blocks[0, 0]
    lists = block_list[0, 0]
    count = block_count[0, 0]
    target = lists[:, 0] * clus
    source = lists[:, 1] * rows + lists[:, 2] * clus

    def fold_slabs(acc, piece):
        length = piece.shape[0]
        for slot in range(slots):
            offset = source[slot]
            valid = (slot < count) & (offset >= 0) & (offset < length)

            def fold_apply(total, slot=slot, offset=offset):
                part = lax.dynamic_slice_in_dim(piece, offset, clus, 0)
                term = jnp.dot(local_blocks[slot], part, preferred_element_type=jnp.float32)
                current = lax.dynamic_slice_in_dim(total, target[slot], clus, 0)
                return lax.dynamic_update_slice_in_dim(total, current + term, target[slot], 0)

            acc = lax.cond(valid, fold_apply, lambda total: total, acc)
        return acc

    empty = jnp.zeros((rows, width), jnp.float32)
    z1 = jnp.dot(features[0], w_in, preferred_element_type=jnp.float32).astype(jnp.bfloat16)
    p1 = fold_slabs(empty, lax.all_gather(z1, "dom", axis=0, tiled=True))
    h1 = jax.nn.gelu(p1, approximate=True).astype(jnp.bfloat16)
    partial_hidden = jnp.dot(h1, w_hidden, preferred_element_type=jnp.float32)
    z2 = lax.psum_scatter(partial_hidden, "col", scatter_dimension=1, tiled=True).astype(
        jnp.bfloat16
    )
    p2 = fold_slabs(empty, lax.all_gather(z2, "dom", axis=0, tiled=True))
    upstream = cotangent[0]
    term_rows = jnp.zeros((rows * lax.axis_size("dom"), width), jnp.float32)
    for slot in range(slots):
        offset = source[slot]
        valid = (slot < count) & (offset >= 0) & (offset < rows * lax.axis_size("dom"))

        def spread_apply(total, slot=slot, offset=offset):
            part = lax.dynamic_slice_in_dim(upstream, target[slot], clus, 0)
            term = lax.dot_general(
                local_blocks[slot],
                part,
                (((0,), (0,)), ((), ())),
                preferred_element_type=jnp.float32,
            )
            current = lax.dynamic_slice_in_dim(total, offset, clus, 0)
            return lax.dynamic_update_slice_in_dim(total, current + term, offset, 0)

        term_rows = lax.cond(valid, spread_apply, lambda total: total, term_rows)
    dz2 = lax.psum_scatter(term_rows, "dom", scatter_dimension=0, tiled=True).astype(jnp.bfloat16)
    local_grad = lax.dot_general(
        h1,
        lax.all_gather(dz2, "col", axis=1, tiled=True),
        (((0,), (0,)), ((), ())),
        preferred_element_type=jnp.float32,
    )
    grad = lax.psum_scatter(local_grad, ("dom", "rep"), scatter_dimension=1, tiled=True)
    return (p2.astype(jnp.bfloat16)[None], grad)


def solution(mesh):
    placed = (
        P("rep", "dom", None),
        P(None, "col"),
        P("col", None),
        P("rep", "dom", None, None, None),
        P("rep", "dom", None, None),
        P("rep", "dom"),
        P("rep", "dom", "col"),
    )
    return jax.shard_map(
        body,
        mesh=mesh,
        in_specs=placed,
        out_specs=(P("rep", "dom", "col"), P("col", ("dom", "rep"))),
        check_vma=False,
    )
```

profile of v0, /device:TPU:26, one launch (start us, length us, event | category | flops | bytes accessed | tf_op | source)
XLA Modules:
  0.0 273.7 jit_solution(215742913712855361)
XLA Ops:
  20.2 6.1 %conditional.40 = (f32[4096,64]{0,1:T(8,128)}) conditional(s32[]{:T(128)} %convert_element_type.68, () %tuple.190, (s32[8]{0:T(128)S(1)}, bf16[1024,64]{1,0:T(8,128)(2,1)S(1)}, bf16[8,512,512]{2,1,0:T(8,128)(2,1)}, s32[]{:T(128)}) %tuple.302), branch_computations={%region_33.0_spmd, %region_34.0_spmd} | conditional | flops 33554436 | bytes 2097240 | solution.py:59
  24.6 1.6 dynamic_update_slice.64
  26.2 7.5 %conditional.41 = (f32[4096,64]{0,1:T(8,128)}) conditional(s32[]{:T(128)} %convert_element_type.67, f32[4096,64]{0,1:T(8,128)} %get-tuple-element.562, (s32[]{:T(128)}, f32[4096,64]{0,1:T(8,128)}, s32[8]{0:T(128)S(1)}, bf16[1024,64]{1,0:T(8,128)(2,1)S(1)}, bf16[8,512,512]{2,1,0:T(8,128)(2,1)}) %tuple.303), branch_computations={%region_35.0_spmd, %region_36.0_spmd} | conditional | flops 33587208 | bytes 1179744 | solution.py:59
  32.0 1.7 dynamic_update_slice.65
  33.7 7.3 %conditional.42 = (f32[4096,64]{0,1:T(8,128)}) conditional(s32[]{:T(128)} %convert_element_type.66, f32[4096,64]{0,1:T(8,128)} %get-tuple-element.563, (s32[]{:T(128)}, f32[4096,64]{0,1:T(8,128)}, s32[8]{0:T(128)S(1)}, bf16[1024,64]{1,0:T(8,128)(2,1)S(1)}, bf16[8,512,512]{2,1,0:T(8,128)(2,1)}) %tuple.304), branch_computations={%region_37.0_spmd, %region_38.0_spmd} | conditional | flops 33587208 | bytes 1179744 | solution.py:59
  39.3 1.7 dynamic_update_slice.66
  41.0 7.6 %conditional.43 = (f32[4096,64]{0,1:T(8,128)}) conditional(s32[]{:T(128)} %convert_element_type.65, f32[4096,64]{0,1:T(8,128)} %get-tuple-element.564, (s32[]{:T(128)}, f32[4096,64]{0,1:T(8,128)}, s32[8]{0:T(128)S(1)}, bf16[1024,64]{1,0:T(8,128)(2,1)S(1)}, bf16[8,512,512]{2,1,0:T(8,128)(2,1)}) %tuple.305), branch_computations={%region_39.0_spmd, %region_40.0_spmd} | conditional | flops 33587208 | bytes 1179744 | solution.py:59
  46.9 1.7 dynamic_update_slice.67
  48.6 7.4 %conditional.44 = (f32[4096,64]{0,1:T(8,128)}) conditional(s32[]{:T(128)} %convert_element_type.64, f32[4096,64]{0,1:T(8,128)} %get-tuple-element.565, (s32[]{:T(128)}, f32[4096,64]{0,1:T(8,128)}, s32[8]{0:T(128)S(1)}, bf16[1024,64]{1,0:T(8,128)(2,1)S(1)}, bf16[8,512,512]{2,1,0:T(8,128)(2,1)}) %tuple.306), branch_computations={%region_41.0_spmd, %region_42.0_spmd} | conditional | flops 33587208 | bytes 1179744 | solution.py:59
  54.3 1.7 dynamic_update_slice.68
  56.0 7.4 %conditional.45 = (f32[4096,64]{0,1:T(8,128)}) conditional(s32[]{:T(128)} %convert_element_type.63, f32[4096,64]{0,1:T(8,128)} %get-tuple-element.566, (s32[]{:T(128)}, f32[4096,64]{0,1:T(8,128)}, s32[8]{0:T(128)S(1)}, bf16[1024,64]{1,0:T(8,128)(2,1)S(1)}, bf16[8,512,512]{2,1,0:T(8,128)(2,1)}) %tuple.307), branch_computations={%region_43.0_spmd, %region_44.0_spmd} | conditional | flops 33587208 | bytes 1179744 | solution.py:59
  61.7 1.7 dynamic_update_slice.69
  63.4 7.2 %conditional.46 = (f32[4096,64]{0,1:T(8,128)}) conditional(s32[]{:T(128)} %convert_element_type.62, f32[4096,64]{0,1:T(8,128)} %get-tuple-element.567, (s32[]{:T(128)}, f32[4096,64]{0,1:T(8,128)}, s32[8]{0:T(128)S(1)}, bf16[1024,64]{1,0:T(8,128)(2,1)S(1)}, bf16[8,512,512]{2,1,0:T(8,128)(2,1)}) %tuple.308), branch_computations={%region_45.0_spmd, %region_46.0_spmd} | conditional | flops 33587208 | bytes 1179744 | solution.py:59
  68.9 1.7 dynamic_update_slice.70
  70.6 7.2 %conditional.47 = (f32[4096,64]{0,1:T(8,128)}) conditional(s32[]{:T(128)} %convert_element_type.61, f32[4096,64]{0,1:T(8,128)} %get-tuple-element.568, (s32[]{:T(128)}, f32[4096,64]{0,1:T(8,128)}, s32[8]{0:T(128)S(1)}, bf16[1024,64]{1,0:T(8,128)(2,1)S(1)}, bf16[8,512,512]{2,1,0:T(8,128)(2,1)}) %tuple.309), branch_computations={%region_47.0_spmd, %region_48.0_spmd} | conditional | flops 33587208 | bytes 1179744 | solution.py:59
  76.1 1.7 dynamic_update_slice.71
  78.1 19.9 %all_gather.9 = bf16[4096,64]{0,1:T(8,128)(2,1)S(1)} all-gather(bf16[1024,64]{0,1:T(8,128)(2,1)S(1)} %convolution_convert_fusion), channel_id=1, replica_groups=mesh['dom'=4,'col'=4,'rep'=2] {'dom'}, dimensions={0}, use_global_device_ids=true | all-gather | bytes 655360 | tf_op jit(solution)/shard_map/all_gather | solution.py:35
  98.0 6.2 %conditional.24 = (f32[1024,64]{0,1:T(8,128)}) conditional(s32[]{:T(128)} %convert_element_type.68, () %tuple.173, (s32[]{:T(128)}, bf16[4096,64]{0,1:T(8,128)(2,1)S(1)}, bf16[8,512,512]{2,1,0:T(8,128)(2,1)}, s32[8]{0:T(128)S(1)}) %tuple.286), branch_computations={%region_0.0_spmd, %region_1.0_spmd} | conditional | flops 33554436 | bytes 2359384 | solution.py:30
  104.1 7.9 %conditional.25 = (f32[1024,64]{0,1:T(8,128)}) conditional(s32[]{:T(128)} %convert_element_type.67, f32[1024,64]{0,1:T(8,128)} %get-tuple-element.546, (s32[8]{0:T(128)S(1)}, f32[1024,64]{0,1:T(8,128)}, s32[]{:T(128)}, bf16[4096,64]{0,1:T(8,128)(2,1)S(1)}, bf16[8,512,512]{2,1,0:T(8,128)(2,1)}) %tuple.287), branch_computations={%region_2.0_spmd, %region_3.0_spmd} | conditional | flops 33587208 | bytes 2228320 | solution.py:30
  112.0 7.8 %conditional.26 = (f32[1024,64]{0,1:T(8,128)}) conditional(s32[]{:T(128)} %convert_element_type.66, f32[1024,64]{0,1:T(8,128)} %get-tuple-element.547, (s32[8]{0:T(128)S(1)}, f32[1024,64]{0,1:T(8,128)}, s32[]{:T(128)}, bf16[4096,64]{0,1:T(8,128)(2,1)S(1)}, bf16[8,512,512]{2,1,0:T(8,128)(2,1)}) %tuple.288), branch_computations={%region_4.0_spmd, %region_5.0_spmd} | conditional | flops 33587208 | bytes 2228320 | solution.py:30
  118.1 1.7 dynamic_update_slice.50
  119.8 8.0 %conditional.27 = (f32[1024,64]{0,1:T(8,128)}) conditional(s32[]{:T(128)} %convert_element_type.65, f32[1024,64]{0,1:T(8,128)} %get-tuple-element.548, (s32[8]{0:T(128)S(1)}, f32[1024,64]{0,1:T(8,128)}, s32[]{:T(128)}, bf16[4096,64]{0,1:T(8,128)(2,1)S(1)}, bf16[8,512,512]{2,1,0:T(8,128)(2,1)}) %tuple.289), branch_computations={%region_6.0_spmd, %region_7.0_spmd} | conditional | flops 33587208 | bytes 2228320 | solution.py:30
  127.8 7.9 %conditional.28 = (f32[1024,64]{0,1:T(8,128)}) conditional(s32[]{:T(128)} %convert_element_type.64, f32[1024,64]{0,1:T(8,128)} %get-tuple-element.549, (s32[8]{0:T(128)S(1)}, f32[1024,64]{0,1:T(8,128)}, s32[]{:T(128)}, bf16[4096,64]{0,1:T(8,128)(2,1)S(1)}, bf16[8,512,512]{2,1,0:T(8,128)(2,1)}) %tuple.290), branch_computations={%region_8.0_spmd, %region_9.0_spmd} | conditional | flops 33587208 | bytes 2228320 | solution.py:30
  134.0 1.7 dynamic_update_slice.52
  135.7 7.9 %conditional.29 = (f32[1024,64]{0,1:T(8,128)}) conditional(s32[]{:T(128)} %convert_element_type.63, f32[1024,64]{0,1:T(8,128)} %get-tuple-element.550, (s32[8]{0:T(128)S(1)}, f32[1024,64]{0,1:T(8,128)}, s32[]{:T(128)}, bf16[4096,64]{0,1:T(8,128)(2,1)S(1)}, bf16[8,512,512]{2,1,0:T(8,128)(2,1)}) %tuple.291), branch_computations={%region_10.0_spmd, %region_11.0_spmd} | conditional | flops 33587208 | bytes 2228320 | solution.py:30
  141.9 1.7 dynamic_update_slice.53
  143.6 7.8 %conditional.30 = (f32[1024,64]{0,1:T(8,128)}) conditional(s32[]{:T(128)} %convert_element_type.62, f32[1024,64]{0,1:T(8,128)} %get-tuple-element.551, (s32[8]{0:T(128)S(1)}, f32[1024,64]{0,1:T(8,128)}, s32[]{:T(128)}, bf16[4096,64]{0,1:T(8,128)(2,1)S(1)}, bf16[8,512,512]{2,1,0:T(8,128)(2,1)}) %tuple.292), branch_computations={%region_12.0_spmd, %region_13.0_spmd} | conditional | flops 33587208 | bytes 2228320 | solution.py:30
  149.7 1.7 dynamic_update_slice.54
  151.3 7.6 %conditional.31 = (f32[1024,64]{0,1:T(8,128)}) conditional(s32[]{:T(128)} %convert_element_type.61, f32[1024,64]{0,1:T(8,128)} %get-tuple-element.552, (s32[8]{0:T(128)S(1)}, f32[1024,64]{0,1:T(8,128)}, s32[]{:T(128)}, bf16[4096,64]{0,1:T(8,128)(2,1)S(1)}, bf16[8,512,512]{2,1,0:T(8,128)(2,1)}) %tuple.293), branch_computations={%region_14.0_spmd, %region_15.0_spmd} | conditional | flops 33587208 | bytes 2228320 | solution.py:30
  158.9 2.3 fusion.128
  162.3 7.2 %all_gather.11 = bf16[1024,256]{0,1:T(8,128)(2,1)S(1)} all-gather(bf16[1024,64]{0,1:T(8,128)(2,1)S(1)} %convert_element_type.73), channel_id=1, replica_groups=mesh['dom'=4,'col'=4,'rep'=2] {'col'}, dimensions={1}, use_global_device_ids=true | all-gather | bytes 655360 | tf_op jit(solution)/shard_map/all_gather | solution.py:63
  169.5 1.9 fusion.126
  171.5 15.7 %reduce-scatter.4.cloned.1.call-done = f32[1024,64]{0,1:T(8,128)} async-done(((f32[1024,256]{0,1:T(8,128)}), f32[1024,64]{0,1:T(8,128)}) %reduce-scatter.4.cloned.1.call-update) | async-done | bytes 262160 | tf_op jit(solution)/shard_map/reduce_scatter | solution.py:38
  188.2 16.3 %all_gather.10 = bf16[4096,64]{0,1:T(8,128)(2,1)S(1)} all-gather(bf16[1024,64]{0,1:T(8,128)(2,1)S(1)} %convert_element_type.71), channel_id=1, replica_groups=mesh['dom'=4,'col'=4,'rep'=2] {'dom'}, dimensions={0}, use_global_device_ids=true | all-gather | bytes 655360 | tf_op jit(solution)/shard_map/all_gather | solution.py:41
  204.5 6.2 %conditional.32 = (f32[1024,64]{0,1:T(8,128)}) conditional(s32[]{:T(128)} %convert_element_type.68, () %tuple.172, (s32[]{:T(128)}, bf16[4096,64]{0,1:T(8,128)(2,1)S(1)}, bf16[8,512,512]{2,1,0:T(8,128)(2,1)}, s32[8]{0:T(128)S(1)}) %tuple.294), branch_computations={%region_17.0_spmd, %region_18.0_spmd} | conditional | flops 33554436 | bytes 2359384 | solution.py:30
  210.7 7.9 %conditional.33 = (f32[1024,64]{0,1:T(8,128)}) conditional(s32[]{:T(128)} %convert_element_type.67, f32[1024,64]{0,1:T(8,128)} %get-tuple-element.554, (s32[8]{0:T(128)S(1)}, f32[1024,64]{0,1:T(8,128)}, s32[]{:T(128)}, bf16[4096,64]{0,1:T(8,128)(2,1)S(1)}, bf16[8,512,512]{2,1,0:T(8,128)(2,1)}) %tuple.295), branch_computations={%region_19.0_spmd, %region_20.0_spmd} | conditional | flops 33587208 | bytes 2228320 | solution.py:30
  217.0 1.6 dynamic_update_slice.57
  218.6 7.8 %conditional.34 = (f32[1024,64]{0,1:T(8,128)}) conditional(s32[]{:T(128)} %convert_element_type.66, f32[1024,64]{0,1:T(8,128)} %get-tuple-element.555, (s32[8]{0:T(128)S(1)}, f32[1024,64]{0,1:T(8,128)}, s32[]{:T(128)}, bf16[4096,64]{0,1:T(8,128)(2,1)S(1)}, bf16[8,512,512]{2,1,0:T(8,128)(2,1)}) %tuple.296), branch_computations={%region_21.0_spmd, %region_22.0_spmd} | conditional | flops 33587208 | bytes 2228320 | solution.py:30
  224.7 1.7 dynamic_update_slice.58
  226.3 8.0 %conditional.35 = (f32[1024,64]{0,1:T(8,128)}) conditional(s32[]{:T(128)} %convert_element_type.65, f32[1024,64]{0,1:T(8,128)} %get-tuple-element.556, (s32[8]{0:T(128)S(1)}, f32[1024,64]{0,1:T(8,128)}, s32[]{:T(128)}, bf16[4096,64]{0,1:T(8,128)(2,1)S(1)}, bf16[8,512,512]{2,1,0:T(8,128)(2,1)}) %tuple.297), branch_computations={%region_23.0_spmd, %region_24.0_spmd} | conditional | flops 33587208 | bytes 2228320 | solution.py:30
  234.4 7.9 %conditional.36 = (f32[1024,64]{0,1:T(8,128)}) conditional(s32[]{:T(128)} %convert_element_type.64, f32[1024,64]{0,1:T(8,128)} %get-tuple-element.557, (s32[8]{0:T(128)S(1)}, f32[1024,64]{0,1:T(8,128)}, s32[]{:T(128)}, bf16[4096,64]{0,1:T(8,128)(2,1)S(1)}, bf16[8,512,512]{2,1,0:T(8,128)(2,1)}) %tuple.298), branch_computations={%region_25.0_spmd, %region_26.0_spmd} | conditional | flops 33587208 | bytes 2228320 | solution.py:30
  240.6 1.7 dynamic_update_slice.60
  242.3 7.9 %conditional.37 = (f32[1024,64]{0,1:T(8,128)}) conditional(s32[]{:T(128)} %convert_element_type.63, f32[1024,64]{0,1:T(8,128)} %get-tuple-element.558, (s32[8]{0:T(128)S(1)}, f32[1024,64]{0,1:T(8,128)}, s32[]{:T(128)}, bf16[4096,64]{0,1:T(8,128)(2,1)S(1)}, bf16[8,512,512]{2,1,0:T(8,128)(2,1)}) %tuple.299), branch_computations={%region_27.0_spmd, %region_28.0_spmd} | conditional | flops 33587208 | bytes 2228320 | solution.py:30
  248.5 1.7 dynamic_update_slice.61
  250.2 7.8 %conditional.38 = (f32[1024,64]{0,1:T(8,128)}) conditional(s32[]{:T(128)} %convert_element_type.62, f32[1024,64]{0,1:T(8,128)} %get-tuple-element.559, (s32[8]{0:T(128)S(1)}, f32[1024,64]{0,1:T(8,128)}, s32[]{:T(128)}, bf16[4096,64]{0,1:T(8,128)(2,1)S(1)}, bf16[8,512,512]{2,1,0:T(8,128)(2,1)}) %tuple.300), branch_computations={%region_29.0_spmd, %region_30.0_spmd} | conditional | flops 33587208 | bytes 2228320 | solution.py:30
  256.3 1.7 dynamic_update_slice.62
  258.0 7.6 %conditional.39 = (f32[1024,64]{0,1:T(8,128)}) conditional(s32[]{:T(128)} %convert_element_type.61, f32[1024,64]{0,1:T(8,128)} %get-tuple-element.560, (s32[8]{0:T(128)S(1)}, f32[1024,64]{0,1:T(8,128)}, s32[]{:T(128)}, bf16[4096,64]{0,1:T(8,128)(2,1)S(1)}, bf16[8,512,512]{2,1,0:T(8,128)(2,1)}) %tuple.301), branch_computations={%region_31.0_spmd, %region_32.0_spmd} | conditional | flops 33587208 | bytes 2228320 | solution.py:30
  265.6 1.6 convert_bitcast_fusion
  (92 shorter events, 70.4 us)
Async XLA Ops:
  7.2 70.7 %copy-start = (bf16[1,1024,100]{1,2,0:T(8,128)(2,1)S(1)}, bf16[1,1024,100]{1,2,0:T(8,128)(2,1)}, u32[]{:S(2)}) copy-start(bf16[1,1024,100]{1,2,0:T(8,128)(2,1)} %param.55) | copy-start | bytes 614404
  7.2 154.1 %reduce-scatter.6.cloned.1.call-start = ((), (), s32[]{:S(2)}) async-start(), calls=%async_computation.4 | async-start | bytes 1310720 | tf_op jit(solution)/shard_map/reduce_scatter | solution.py:60
  33.7 44.2 %copy-start.2 = (bf16[100,64]{0,1:T(8,128)(2,1)S(1)}, bf16[100,64]{0,1:T(8,128)(2,1)}, u32[]{:S(2)}) copy-start(bf16[100,64]{0,1:T(8,128)(2,1)} %param.56) | copy-start | bytes 38404
  77.8 109.4 %reduce-scatter.4.cloned.1.call-start = ((), (), s32[]{:S(2)}) async-start(), calls=%async_computation.3 | async-start | bytes 1310720 | tf_op jit(solution)/shard_map/reduce_scatter | solution.py:38
  135.7 23.3 %copy-start.1 = (bf16[64,256]{1,0:T(8,128)(2,1)S(1)}, bf16[64,256]{1,0:T(8,128)(2,1)}, u32[]{:S(2)}) copy-start(bf16[64,256]{1,0:T(8,128)(2,1)} %param.57) | copy-start | bytes 98308
  161.2 106.0 %reduce-scatter.8.cloned.1.call-start = ((), (), s32[]{:S(2)}) async-start(), calls=%async_computation.5 | async-start | bytes 147456 | tf_op jit(solution)/shard_map/reduce_scatter | solution.py:67
Sparse Core Ops, SparseCore 0:
  77.9 31.2 reduce-scatter.5
  161.4 25.8 reduce-scatter.3
  191.1 59.9 reduce-scatter.7
where the time goes:
time: 277 us; the launch traced here: 274 us
  loops' own time  85.5 us (31%)
  local copies, waits for them, and re-layouts  64.4 us (23%)
  blocking collectives  43.5 us (16%)
  matrix products  36.6 us (13%)
  between operations  24.3 us (9%)
  waiting for transfers between devices  15.8 us (6%)
  other arithmetic  3.56 us (1%)
    another operation x16, loops' own time, fold_slabs(): acc = lax.cond(valid, fold_apply, lambda total: total, acc)  57 us
    another operation x8, loops' own time, body(): term_rows = lax.cond(valid, spread_apply, lambda total: total, term_rows)  28.5 us
    dynamic_update_slice x16, local copies, waits for them, and re-layouts, fold_apply(): lax.dynamic_update_slice_in_dim(total, current + term, target[slot], 0)  26.1 us
    dot_general x16, matrix products, fold_apply(): term = jnp.dot(local_blocks[slot], part, preferred_element_type=jnp.float32)  21.7 us
    all_gather x1, blocking collectives, body(): p1 = fold_slabs(empty, lax.all_gather(z1, 'dom', axis=0, tiled=True))  19.9 us
    all_gather x1, blocking collectives, body(): p2 = fold_slabs(empty, lax.all_gather(z2, 'dom', axis=0, tiled=True))  16.3 us
    reduce_scatter x1, waiting for transfers between devices, body(): lax.psum_scatter(partial_hidden, 'col', scatter_dimension=1, tiled=True)  15.7 us
    dynamic_update_slice x8, local copies, waits for them, and re-layouts, spread_apply(): return lax.dynamic_update_slice_in_dim(total, current + term, offset, 0)  13.5 us
  transfers between devices with their start and end apart: 3, of which 1 were waited for; matrix products, arithmetic and copies ran while one was open for 27% of the time, Pallas kernels for 0%

commit v1 on v0

v1 whole, which is shorter than its diff:
```python
import functools
import math

import jax
import jax.numpy as jnp
from jax import lax
from jax.experimental import pallas as pl
from jax.experimental.pallas import tpu as pltpu
from jax.sharding import PartitionSpec as P


BF = jnp.bfloat16
F32 = jnp.float32
VM = pl.BlockSpec(memory_space=pltpu.VMEM)
SM = pl.BlockSpec(memory_space=pltpu.SMEM)
HB = pl.BlockSpec(memory_space=pltpu.HBM)
LANES = 128
LIM = 24 << 20
SPREAD_LIM = 50 << 20
ROWS = 16


def dot(a, b):
    return jnp.dot(a, b, preferred_element_type=F32)


def call(kernel, ins, specs, outs, scratch=(), flops=0, limit=24 << 20):
    return pl.pallas_call(
        kernel,
        out_shape=outs,
        in_specs=specs,
        out_specs=jax.tree.map(lambda _: VM, outs),
        scratch_shapes=list(scratch),
        compiler_params=pltpu.CompilerParams(vmem_limit_bytes=limit),
        cost_estimate=pl.CostEstimate(flops=flops, bytes_accessed=1 << 20, transcendentals=0),
    )(*ins)


def tables(lst, cnt, lst_s, cnt_s, sems):
    return [pltpu.make_async_copy(lst, lst_s, sems.at[0]), pltpu.make_async_copy(cnt, cnt_s, sems.at[1])]


def ndot(a, b):
    return lax.dot_general(a, b, (((1,), (1,)), ((), ())), preferred_element_type=F32)


def onehot(mask):
    return mask.astype(F32).astype(BF)


def pack_kernel(feats_h, w_in_h, w_hid_h, xp, *refs, n_col, per, lane):
    wps = refs[:n_col]
    feats, w_in, w_hid, h_abs, sems = refs[n_col:]
    pairs = ((feats_h, feats), (w_in_h, w_in), (w_hid_h, w_hid))
    copies = [pltpu.make_async_copy(a, b, sems.at[n]) for n, (a, b) in enumerate(pairs)]
    for copy in copies:
        copy.start()
    c = lax.axis_index("col")
    n_feat = feats.shape[1]
    width = w_in.shape[0]
    row = lax.broadcasted_iota(jnp.int32, (lane, n_feat), 0)
    col = lax.broadcasted_iota(jnp.int32, (lane, n_feat), 1)
    mine = onehot((row < per) & (col == c * per + row))
    frow = lax.broadcasted_iota(jnp.int32, (n_feat, LANES), 0)
    fcol = lax.broadcasted_iota(jnp.int32, (n_feat, LANES), 1)
    inner = lax.rem(fcol, lane)
    every = onehot((inner < per) & (frow == (fcol // lane) * per + inner))
    for copy in copies:
        copy.wait()
    xp[...] = dot(mine, feats[0]).astype(BF)
    spread = dot(w_in[...], every).astype(BF)
    turned = w_hid[...].astype(F32).T.astype(BF)
    for t in range(n_col):
        h_abs[t] = turned[t * width : (t + 1) * width, :]
    for t in range(n_col):
        part = h_abs[lax.rem(c + t, n_col)]
        wps[t][...] = jnp.zeros(wps[t].shape, BF)
        for m in range(width // ROWS):
            rows = slice(m * ROWS, (m + 1) * ROWS)
            wps[t][:, 2 * m * LANES : (2 * m + 1) * LANES] = spread[rows, :]
            wps[t][:, (2 * m + 1) * LANES : (2 * m + 1) * LANES + width] = part[rows, :]


def spread_kernel(lst_h, cnt_h, cot_h, blocks, *refs, n_dom, slots, clus, width):
    outs = refs[:n_dom]
    lst, cnt, cot, held, acc, small, sems = refs[n_dom:]
    first = tables(lst_h, cnt_h, lst, cnt, small) + [pltpu.make_async_copy(cot_h, cot, small.at[2])]
    copies = [pltpu.make_async_copy(blocks.at[0, 0, k], held.at[k], sems.at[k]) for k in range(slots)]
    for copy in first + copies:
        copy.start()
    p = lax.axis_index("dom")
    cl = acc.shape[0] // n_dom
    acc[...] = jnp.zeros(acc.shape, F32)
    for copy in first:
        copy.wait()
    for k in range(slots):
        i = jnp.clip(lst[0, 0, 0, k], 0, cl - 1)
        at = lax.rem(lst[0, 1, 0, k] - p + n_dom, n_dom) * cl + lst[0, 2, 0, k]
        at = jnp.clip(at, 0, n_dom * cl - 1)
        left = cot[0, :, pl.ds(pl.multiple_of(i * clus, LANES), clus)]
        left = jnp.where(k < cnt[0, 0], left, jnp.zeros_like(left))
        copies[k].wait()
        acc[at] += dot(left, held[k])
    for s in range(n_dom):
        for j in range(cl):
            outs[s][:, j * clus : (j + 1) * clus] = acc[s * cl + j].astype(outs[s].dtype)


def fold(lst_h, cnt_h, held, lst, cnt, src, acc, small, fill, n_dom, slots):
    first = tables(lst_h, cnt_h, lst, cnt, small)
    for copy in first:
        copy.start()
    cl = acc.shape[0]
    p = lax.axis_index("dom")
    fill()
    acc[...] = jnp.zeros(acc.shape, F32)
    for copy in first:
        copy.wait()
    for k in range(slots):
        i = jnp.clip(lst[0, 0, 0, k], 0, cl - 1)
        at = lax.rem(p - lst[0, 1, 0, k] + n_dom, n_dom) * cl + lst[0, 2, 0, k]
        left = src[jnp.clip(at, 0, n_dom * cl - 1)]
        left = jnp.where(k < cnt[0, 0], left, jnp.zeros_like(left))
        acc[i] += ndot(left, held[0, 0, k])


def first_kernel(lst_h, cnt_h, held, *refs, n_dom, n_col, slots, clus, cl, lane):
    xs = refs[:n_dom]
    wps = refs[n_dom : n_dom + n_col]
    outs = refs[n_dom + n_col : n_dom + 2 * n_col]
    lst, cnt, src, acc, small = refs[n_dom + 2 * n_col :]

    def fill():
        for s in range(n_dom):
            for j in range(cl):
                src[s * cl + j] = xs[s][:, j * clus : (j + 1) * clus]
        for t in range(n_col):
            outs[t][lane:, :] = wps[t][...]

    fold(lst_h, cnt_h, held, lst, cnt, src, acc, small, fill, n_dom, slots)
    for i in range(cl):
        part = acc[i].astype(BF)
        for t in range(n_col):
            outs[t][:lane, i * clus : (i + 1) * clus] = part


def gelu(v):
    return 0.5 * v * (1.0 + jnp.tanh(math.sqrt(2.0 / math.pi) * (v + 0.044715 * v * v * v)))


def hidden_kernel(*refs, n_col, lane, width):
    pays = refs[:n_col]
    h1, zp, ax, w1, w2 = refs[n_col:]
    c = lax.axis_index("col")
    for t in range(n_col):
        frm = lax.rem(c - t + n_col, n_col)
        ax[frm] = pays[t][:lane, :]
        for m in range(width // ROWS):
            rows = slice(m * ROWS, (m + 1) * ROWS)
            w1[frm, rows, :] = pays[t][lane:, 2 * m * LANES : (2 * m + 1) * LANES]
            w2[frm, rows, :] = pays[t][lane:, (2 * m + 1) * LANES : (2 * m + 1) * LANES + width]
    left = w1[...].reshape(n_col * width, LANES)
    out = jnp.concatenate([w2[t] for t in range(n_col)], axis=1)
    nodes = h1.shape[1]
    right = ax[...].reshape(n_col * lane, nodes)
    step = nodes // 4
    for m in range(4):
        cols = slice(m * step, (m + 1) * step)
        h = gelu(dot(left, right[:, cols])).astype(BF)
        h1[:, cols] = h
        zp[:, cols] = dot(out, h).astype(BF)


def grad_kernel(*refs, n_dom, n_rep, wj):
    ys = refs[:n_dom]
    h1 = refs[n_dom]
    outs = refs[n_dom + 1 : -1]
    store = refs[-1]
    r = lax.axis_index("rep")
    total = ys[0][...]
    for y in ys[1:]:
        total = total + y[...].astype(F32)
    g = ndot(total.astype(BF), h1[...])
    for b in range(n_rep):
        store[b] = g[b * wj : (b + 1) * wj, :]
    for b in range(n_rep):
        outs[b][...] = store[lax.rem(r + b, n_rep)]


def pieces_kernel(*refs, n_col, n_rep, width, packs):
    parts = refs[:n_rep]
    outs = refs[n_rep:-1]
    store = refs[-1]
    d = lax.axis_index("dom")
    g = parts[0][...]
    for part in parts[1:]:
        g = g + part[...]
    rows = g.shape[0] // packs
    for t in range(n_col):
        for m in range(packs):
            store[t, :, m * width : (m + 1) * width] = g[m * rows : (m + 1) * rows, t * width : (t + 1) * width]
    for a in range(n_col):
        outs[a][...] = store[lax.rem(d + a, n_col)]


def second_kernel(lst_h, cnt_h, held, *refs, n_dom, slots, clus, cl):
    zs = refs[:n_dom]
    out, lst, cnt, src, acc, small = refs[n_dom:]

    def fill():
        for s in range(n_dom):
            for j in range(cl):
                src[s * cl + j] = zs[s][:, j * clus : (j + 1) * clus]

    fold(lst_h, cnt_h, held, lst, cnt, src, acc, small, fill, n_dom, slots)
    for i in range(cl):
        out[0, :, i * clus : (i + 1) * clus] = acc[i].astype(BF)


def sum_kernel(*refs, packs, width):
    pieces = refs[:-1]
    out = refs[-1]
    total = pieces[0][...]
    for piece in pieces[1:]:
        total = total + piece[...]
    rows = total.shape[0]
    for m in range(packs):
        out[m * rows : (m + 1) * rows, :] = total[:, m * width : (m + 1) * width]


def shifted(x, axis, size, s):
    return lax.ppermute(x, axis, [(i, (i + s) % size) for i in range(size)])


def body(features, w_in, w_hidden, blocks, block_list, block_count, cotangent):
    n_dom, n_col, n_rep = lax.axis_size("dom"), lax.axis_size("col"), lax.axis_size("rep")
    features = jnp.swapaxes(features, 1, 2)
    cotangent = jnp.swapaxes(cotangent, 1, 2)
    w_in = w_in.T
    block_list = jnp.transpose(block_list, (0, 3, 1, 2))
    n_feat, nodes = features.shape[1:]
    slots, clus = blocks.shape[2], blocks.shape[3]
    cl = nodes // clus
    width = w_in.shape[0]
    hid = width * n_col
    per = -(-n_feat // n_col)
    lane = LANES // n_col
    wj = hid // (n_dom * n_rep)
    assert n_dom == n_col and wj * n_rep == width and width % ROWS == 0
    assert per <= lane and lane % ROWS == 0 and width <= LANES and 2 * LANES * (width // ROWS) <= nodes
    packs = LANES // width if wj % (8 * (LANES // width)) == 0 else 1
    sds = jax.ShapeDtypeStruct
    block_flops = 2 * slots * clus * clus

    slot_scratch = [
        pltpu.SMEM(block_list.shape, jnp.int32),
        pltpu.SMEM(block_count.shape, jnp.int32),
    ]
    sems = pltpu.SemaphoreType.DMA((slots,))
    small = pltpu.SemaphoreType.DMA((3,))
    packed = call(
        functools.partial(pack_kernel, n_col=n_col, per=per, lane=lane),
        (features, w_in, w_hidden),
        [HB] * 3,
        [sds((lane, nodes), BF)] + [sds((ROWS, nodes), BF)] * n_col,
        [
            pltpu.VMEM(features.shape, BF),
            pltpu.VMEM(w_in.shape, BF),
            pltpu.VMEM(w_hidden.shape, BF),
            pltpu.VMEM((n_col, width, width), BF),
            small,
        ],
        flops=2 * nodes * n_feat * LANES,
    )
    xs = [packed[0]] + [shifted(packed[0], "dom", n_dom, s) for s in range(1, n_dom)]
    ys = call(
        functools.partial(spread_kernel, n_dom=n_dom, slots=slots, clus=clus, width=width),
        (block_list, block_count, cotangent, blocks),
        [HB] * 4,
        [sds((width, nodes), F32)] + [sds((width, nodes), BF)] * (n_dom - 1),
        slot_scratch + [
            pltpu.VMEM(cotangent.shape, BF),
            pltpu.VMEM((slots, clus, clus), BF),
            pltpu.VMEM((n_dom * cl, width, clus), F32),
            small,
            sems,
        ],
        flops=block_flops * 256,
        limit=SPREAD_LIM,
    )
    ys = [ys[0]] + [shifted(ys[s], "dom", n_dom, s) for s in range(1, n_dom)]

    def fold_scratch(wide):
        return slot_scratch + [
            pltpu.VMEM((n_dom * cl, wide, clus), BF),
            pltpu.VMEM((cl, wide, clus), F32),
            small,
        ]

    pays = call(
        functools.partial(first_kernel, n_dom=n_dom, n_col=n_col, slots=slots, clus=clus, cl=cl, lane=lane),
        (block_list, block_count, blocks, *xs, *packed[1:]),
        [HB] * 2 + [VM] * (1 + n_dom + n_col),
        [sds((lane + ROWS, nodes), BF)] * n_col,
        fold_scratch(lane),
        flops=block_flops * 256,
        limit=LIM,
    )
    pays = [pays[0]] + [shifted(pays[t], "col", n_col, t) for t in range(1, n_col)]
    h1, zp = call(
        functools.partial(hidden_kernel, n_col=n_col, lane=lane, width=width),
        pays,
        [VM] * n_col,
        [sds((hid, nodes), BF), sds((width, nodes), BF)],
        [
            pltpu.VMEM((n_col, lane, nodes), BF),
            pltpu.VMEM((n_col, width, LANES), BF),
            pltpu.VMEM((n_col, width, width), BF),
        ],
        flops=2 * nodes * n_col * LANES * hid * 4,
    )
    zs = [zp] + [shifted(zp, "dom", n_dom, s) for s in range(1, n_dom)]
    halves = call(
        functools.partial(grad_kernel, n_dom=n_dom, n_rep=n_rep, wj=wj),
        (*ys, h1),
        [VM] * (n_dom + 1),
        [sds((wj, hid), F32)] * n_rep,
        [pltpu.VMEM((n_rep, wj, hid), F32)],
        flops=2 * nodes * hid * width * 4,
    )
    halves = [halves[0]] + [shifted(halves[b], "rep", n_rep, b) for b in range(1, n_rep)]
    pieces = call(
        functools.partial(pieces_kernel, n_col=n_col, n_rep=n_rep, width=width, packs=packs),
        halves,
        [VM] * n_rep,
        [sds((wj // packs, packs * width), F32)] * n_col,
        [pltpu.VMEM((n_col, wj // packs, packs * width), F32)],
        flops=1000,
    )
    grads = []
    for a in range(n_col):
        pairs = []
        for d in range(n_dom):
            for c in range(n_col):
                pairs.append((d * n_col + c, c * n_col + (d + a) % n_col))
        grads.append(lax.ppermute(pieces[a], ("dom", "col"), pairs))
    out = call(
        functools.partial(second_kernel, n_dom=n_dom, slots=slots, clus=clus, cl=cl),
        (block_list, block_count, blocks, *zs),
        [HB] * 2 + [VM] * (1 + n_dom),
        sds((1, width, nodes), BF),
        fold_scratch(width),
        flops=block_flops * 256,
        limit=LIM,
    )
    grad = call(
        functools.partial(sum_kernel, packs=packs, width=width),
        grads,
        [VM] * n_col,
        sds((wj, width), F32),
        flops=1000,
    )
    return jnp.swapaxes(out, 1, 2), grad.T


def solution(mesh):
    placed = (
        P("rep", "dom", None),
        P(None, "col"),
        P("col", None),
        P("rep", "dom", None, None, None),
        P("rep", "dom", None, None),
        P("rep", "dom"),
        P("rep", "dom", "col"),
    )

    return jax.shard_map(
        body,
        mesh=mesh,
        in_specs=placed,
        out_specs=(P("rep", "dom", "col"), P("col", ("dom", "rep"))),
        check_vma=False,
    )
```

time: 277 us -> 66.6 us (0.24)
  the two profiles are of different devices: /device:TPU:26 before, /device:TPU:0 now
where the time goes in v1:
time: 66.6 us; the launch traced here: 66.3 us
  starting transfers between devices  38.2 us (57%)
  waiting for transfers between devices  11 us (17%)
  Pallas kernels  10.4 us (16%)
  local copies, waits for them, and re-layouts  5.29 us (8%)
  between operations  1.39 us (2%)
    ppermute x13, starting transfers between devices, shifted(): return lax.ppermute(x, axis, [(i, (i + s) % size) for i in range(size)])  25.8 us
    ppermute x4, starting transfers between devices, body(): grads.append(lax.ppermute(pieces[a], ('dom', 'col'), pairs))  12.4 us
    pallas_call x8, Pallas kernels, call(): pl.pallas_call(kernel, out_shape=outs, in_specs=specs, out_specs=jax.tree...  10.4 us
    ppermute x13, waiting for transfers between devices, shifted(): return lax.ppermute(x, axis, [(i, (i + s) % size) for i in range(size)])  8.34 us
    unnamed x16, local copies, waits for them, and re-layouts  5.29 us
    ppermute x4, waiting for transfers between devices, body(): grads.append(lax.ppermute(pieces[a], ('dom', 'col'), pairs))  2.64 us
  transfers between devices with their start and end apart: 17, of which 6 were waited for; matrix products, arithmetic and copies ran while one was open for 0% of the time, Pallas kernels for 8%

profile of v1, /device:TPU:0, one launch (start us, length us, event | category | flops | bytes accessed | tf_op | source)
XLA Modules:
  0.0 66.3 jit_solution(3444566356349902900)
XLA Ops:
  0.6 0.0 copy-start.7
  0.7 0.9 %copy-done.2 = bf16[1,1024,100]{1,2,0:T(8,128)(2,1)S(1)} copy-done((bf16[1,1024,100]{1,2,0:T(8,128)(2,1)S(1)}, bf16[1,1024,100]{1,2,0:T(8,128)(2,1)}, u32[]{:S(2)}) %copy-start.2) | copy-done | bytes 204824
  1.6 0.8 %copy-done.4 = bf16[64,256]{1,0:T(8,128)(2,1)S(1)} copy-done((bf16[64,256]{1,0:T(8,128)(2,1)S(1)}, bf16[64,256]{1,0:T(8,128)(2,1)}, u32[]{:S(2)}) %copy-start.4) | copy-done | bytes 32792
  2.3 0.7 %copy-done.5 = bf16[100,64]{0,1:T(8,128)(2,1)S(1)} copy-done((bf16[100,64]{0,1:T(8,128)(2,1)S(1)}, bf16[100,64]{0,1:T(8,128)(2,1)}, u32[]{:S(2)}) %copy-start.5) | copy-done | bytes 12824
  3.1 0.5 shard_map.86
  3.6 5.1 %collective-permute-start.2 = (bf16[32,1024]{1,0:T(8,128)(2,1)S(1)}, bf16[32,1024]{1,0:T(8,128)(2,1)S(1)}, u32[]{:S(2)}, u32[]{:S(2)}) collective-permute-start(bf16[32,1024]{1,0:T(8,128)(2,1)S(1)} %get-tuple-element.23.refs_0_), channel_id=1, source_target_pairs={{0,24},{8,0},{16,8},{24,16},{1,25},{9,1},{17,9},{25,17},{2,26},{10... | collective-permute-start | bytes 196616 | tf_op jit(solution)/shard_map/ppermute | solution.py:232
  8.7 0.0 collective-permute-start.1
  8.7 1.0 %collective-permute-start = (bf16[32,1024]{1,0:T(8,128)(2,1)S(1)}, bf16[32,1024]{1,0:T(8,128)(2,1)S(1)}, u32[]{:S(2)}, u32[]{:S(2)}) collective-permute-start(bf16[32,1024]{1,0:T(8,128)(2,1)S(1)} %get-tuple-element.23.refs_0_), channel_id=1, source_target_pairs={{0,8},{8,16},{16,24},{24,0},{1,9},{9,17},{17,25},{25,1},{2,10},{10... | collective-permute-start | bytes 196616 | tf_op jit(solution)/shard_map/ppermute | solution.py:232
  10.4 0.8 %collective-permute-done.2.refs_3_ = bf16[32,1024]{1,0:T(8,128)(2,1)S(1)} collective-permute-done((bf16[32,1024]{1,0:T(8,128)(2,1)S(1)}, bf16[32,1024]{1,0:T(8,128)(2,1)S(1)}, u32[]{:S(2)}, u32[]{:S(2)}) %collective-permute-start.2) | collective-permute-done | bytes 65568 | tf_op jit(solution)/shard_map/ppermute | solution.py:232
  11.2 4.0 %collective-permute-done.1.refs_2_ = bf16[32,1024]{1,0:T(8,128)(2,1)S(1)} collective-permute-done((bf16[32,1024]{1,0:T(8,128)(2,1)S(1)}, bf16[32,1024]{1,0:T(8,128)(2,1)S(1)}, u32[]{:S(2)}, u32[]{:S(2)}) %collective-permute-start.1) | collective-permute-done | bytes 65568 | tf_op jit(solution)/shard_map/ppermute | solution.py:232
  15.2 0.0 collective-permute-done.refs_1_
  15.2 2.2 %copy-done = bf16[1,1,8,512,512]{4,3,2,1,0:T(8,128)(2,1)S(1)} copy-done((bf16[1,1,8,512,512]{4,3,2,1,0:T(8,128)(2,1)S(1)}, bf16[1,1,8,512,512]{4,3,2,1,0:T(8,128)(2,1)}, u32[]{:S(2)}) %copy-start) | copy-done | bytes 4194328
  17.4 0.7 %copy-done.6 = s32[1,1,8,3]{2,1,3,0:T(1,128)S(1)} copy-done((s32[1,1,8,3]{2,1,3,0:T(1,128)S(1)}, s32[1,1,8,3]{2,1,3,0:T(1,128)}, u32[]{:S(2)}) %copy-start.6) | copy-done | bytes 120
  18.1 1.9 %shard_map.87 = (bf16[48,1024]{1,0:T(8,128)(2,1)S(1)}, bf16[48,1024]{1,0:T(8,128)(2,1)S(1)}, bf16[48,1024]{1,0:T(8,128)(2,1)S(1)}, bf16[48,1024]{1,0:T(8,128)(2,1)S(1)}) custom-call(s32[1,3,1,8]{3,2,1,0:T(1,128)S(1)} %bitcast.9, s32[1,1]{1,0:T(1,128)S(6)} %copy.9.cnt_h, bf16[1,1,8,512,512]{4,3,2,1,0:T(8,128)(2,1)S(1)} %copy-done, ...), custom_call_target="tpu_custom_call" | custom-call | flops 1073741824 | bytes 1048576 | tf_op jit(solution)/shard_map/pallas_call | solution.py:28
  20.0 0.1 collective-permute-start.3
  20.1 1.6 %collective-permute-start.4 = (bf16[48,1024]{1,0:T(8,128)(2,1)S(1)}, bf16[48,1024]{1,0:T(8,128)(2,1)S(1)}, u32[]{:S(2)}, u32[]{:S(2)}) collective-permute-start(bf16[48,1024]{1,0:T(8,128)(2,1)S(1)} %get-tuple-element.30), channel_id=1, source_target_pairs={{0,4},{2,6},{4,0},{6,2},{1,5},{3,7},{5,1},{7,3},{8,12},{10,14},{12... | collective-permute-start | bytes 294920 | tf_op jit(solution)/shard_map/ppermute | solution.py:232
  21.7 1.4 %collective-permute-start.5 = (bf16[48,1024]{1,0:T(8,128)(2,1)S(1)}, bf16[48,1024]{1,0:T(8,128)(2,1)S(1)}, u32[]{:S(2)}, u32[]{:S(2)}) collective-permute-start(bf16[48,1024]{1,0:T(8,128)(2,1)S(1)} %get-tuple-element.31), channel_id=1, source_target_pairs={{0,6},{2,0},{4,2},{6,4},{1,7},{3,1},{5,3},{7,5},{8,14},{10,8},{12,... | collective-permute-start | bytes 294920 | tf_op jit(solution)/shard_map/ppermute | solution.py:232
  23.1 3.2 %shard_map.90 = (f32[64,1024]{1,0:T(8,128)S(1)}, bf16[64,1024]{1,0:T(8,128)(2,1)S(1)}, bf16[64,1024]{1,0:T(8,128)(2,1)S(1)}, bf16[64,1024]{1,0:T(8,128)(2,1)S(1)}) custom-call(s32[1,3,1,8]{3,2,1,0:T(1,128)S(1)} %bitcast.10, s32[1,1]{1,0:T(1,128)S(6)} %copy.9.cnt_h, bf16[1,64,1024]{2,1,0:T(8,128)(2,1)S(1)} %bitcast.7, bf16[1,1,8,512,512]{4,3,2,1,0:T(8,128)(2,1)} %blocks.1), custom_call_target="tpu_custom_call" | custom-call | flops 1073741824 | bytes 1048576 | tf_op jit(solution)/shard_map/pallas_call | solution.py:28
  26.3 0.2 collective-permute-start.9
  26.5 2.3 %collective-permute-start.10 = (bf16[64,1024]{1,0:T(8,128)(2,1)S(1)}, bf16[64,1024]{1,0:T(8,128)(2,1)S(1)}, u32[]{:S(2)}, u32[]{:S(2)}) collective-permute-start(bf16[64,1024]{1,0:T(8,128)(2,1)S(1)} %get-tuple-element.35), channel_id=1, source_target_pairs={{0,16},{8,24},{16,0},{24,8},{1,17},{9,25},{17,1},{25,9},{2,18},{10... | collective-permute-start | bytes 393224 | tf_op jit(solution)/shard_map/ppermute | solution.py:232
  28.8 0.0 collective-permute-done.3.refs_1_
  28.8 2.2 %collective-permute-start.11 = (bf16[64,1024]{1,0:T(8,128)(2,1)S(1)}, bf16[64,1024]{1,0:T(8,128)(2,1)S(1)}, u32[]{:S(2)}, u32[]{:S(2)}) collective-permute-start(bf16[64,1024]{1,0:T(8,128)(2,1)S(1)} %get-tuple-element.36), channel_id=1, source_target_pairs={{0,24},{8,0},{16,8},{24,16},{1,25},{9,1},{17,9},{25,17},{2,26},{10... | collective-permute-start | bytes 393224 | tf_op jit(solution)/shard_map/ppermute | solution.py:232
  31.0 0.0 collective-permute-done.4.refs_2_
  31.0 0.0 collective-permute-done.5.refs_3_
  31.0 1.1 %shard_map.88 = (bf16[256,1024]{1,0:T(8,128)(2,1)S(1)}, bf16[64,1024]{1,0:T(8,128)(2,1)S(1)}) custom-call(bf16[48,1024]{1,0:T(8,128)(2,1)S(1)} %get-tuple-element.28.refs_0_, bf16[48,1024]{1,0:T(8,128)(2,1)S(1)} %collective-permute-done.3.refs_1_, bf16[48,1024]{1,0:T(8,128)(2,1)S(1)} %collective-permute-done.4.refs_2_, ...), custom_call_target="tpu_custom_call" | custom-call | flops 1073741824 | bytes 1048576 | tf_op jit(solution)/shard_map/pallas_call | solution.py:28
  32.1 0.1 collective-permute-start.8
  32.2 1.2 %collective-permute-start.7 = (bf16[64,1024]{1,0:T(8,128)(2,1)S(1)}, bf16[64,1024]{1,0:T(8,128)(2,1)S(1)}, u32[]{:S(2)}, u32[]{:S(2)}) collective-permute-start(bf16[64,1024]{1,0:T(8,128)(2,1)S(1)} %get-tuple-element.32.refs_0_), channel_id=1, source_target_pairs={{0,16},{8,24},{16,0},{24,8},{1,17},{9,25},{17,1},{25,9},{2,18},{10... | collective-permute-start | bytes 393224 | tf_op jit(solution)/shard_map/ppermute | solution.py:232
  33.4 1.1 %collective-permute-done.9.refs_1_ = bf16[64,1024]{1,0:T(8,128)(2,1)S(1)} collective-permute-done((bf16[64,1024]{1,0:T(8,128)(2,1)S(1)}, bf16[64,1024]{1,0:T(8,128)(2,1)S(1)}, u32[]{:S(2)}, u32[]{:S(2)}) %collective-permute-start.9) | collective-permute-done | bytes 131104 | tf_op jit(solution)/shard_map/ppermute | solution.py:232
  34.5 9.1 %collective-permute-start.6 = (bf16[64,1024]{1,0:T(8,128)(2,1)S(1)}, bf16[64,1024]{1,0:T(8,128)(2,1)S(1)}, u32[]{:S(2)}, u32[]{:S(2)}) collective-permute-start(bf16[64,1024]{1,0:T(8,128)(2,1)S(1)} %get-tuple-element.32.refs_0_), channel_id=1, source_target_pairs={{0,8},{8,16},{16,24},{24,0},{1,9},{9,17},{17,25},{25,1},{2,10},{10... | collective-permute-start | bytes 393224 | tf_op jit(solution)/shard_map/ppermute | solution.py:232
  43.6 0.0 collective-permute-done.10.refs_2_
  43.6 0.0 collective-permute-done.11.refs_3_
  43.6 0.3 shard_map.91
  43.9 1.6 %collective-permute-start.12 = (f32[32,256]{1,0:T(8,128)S(1)}, f32[32,256]{1,0:T(8,128)S(1)}, u32[]{:S(2)}, u32[]{:S(2)}) collective-permute-start(f32[32,256]{1,0:T(8,128)S(1)} %get-tuple-element.39), channel_id=1, source_target_pairs={{0,1},{1,0},{2,3},{3,2},{4,5},{5,4},{6,7},{7,6},{8,9},{9,8},{10,11... | collective-permute-start | bytes 98312 | tf_op jit(solution)/shard_map/ppermute | solution.py:232
  45.4 2.4 %collective-permute-done.12.refs_1_ = f32[32,256]{1,0:T(8,128)S(1)} collective-permute-done((f32[32,256]{1,0:T(8,128)S(1)}, f32[32,256]{1,0:T(8,128)S(1)}, u32[]{:S(2)}, u32[]{:S(2)}) %collective-permute-start.12) | collective-permute-done | bytes 32800 | tf_op jit(solution)/shard_map/ppermute | solution.py:232
  47.9 0.1 shard_map.92
  47.9 0.7 collective-permute-start.13
  48.6 4.2 %collective-permute-start.14 = (f32[16,128]{1,0:T(8,128)S(1)}, f32[16,128]{1,0:T(8,128)S(1)}, u32[]{:S(2)}, u32[]{:S(2)}) collective-permute-start(f32[16,128]{1,0:T(8,128)S(1)} %get-tuple-element.41), channel_id=1, source_target_pairs={{0,2},{2,10},{4,18},{6,26},{8,4},{10,12},{12,20},{14,28},{16,6},{1... | collective-permute-start | bytes 24584 | tf_op jit(solution)/shard_map/ppermute | solution.py:346
  52.8 0.0 collective-permute-done.13.refs_0_
  52.8 3.1 %collective-permute-start.15 = (f32[16,128]{1,0:T(8,128)S(1)}, f32[16,128]{1,0:T(8,128)S(1)}, u32[]{:S(2)}, u32[]{:S(2)}) collective-permute-start(f32[16,128]{1,0:T(8,128)S(1)} %get-tuple-element.42), channel_id=1, source_target_pairs={{0,4},{2,12},{4,20},{6,28},{8,6},{10,14},{12,22},{14,30},{16,0},{1... | collective-permute-start | bytes 24584 | tf_op jit(solution)/shard_map/ppermute | solution.py:346
  55.9 1.3 %collective-permute-done.14.refs_1_ = f32[16,128]{1,0:T(8,128)S(1)} collective-permute-done((f32[16,128]{1,0:T(8,128)S(1)}, f32[16,128]{1,0:T(8,128)S(1)}, u32[]{:S(2)}, u32[]{:S(2)}) %collective-permute-start.14) | collective-permute-done | bytes 8224 | tf_op jit(solution)/shard_map/ppermute | solution.py:346
  57.2 4.4 %collective-permute-start.16 = (f32[16,128]{1,0:T(8,128)S(1)}, f32[16,128]{1,0:T(8,128)S(1)}, u32[]{:S(2)}, u32[]{:S(2)}) collective-permute-start(f32[16,128]{1,0:T(8,128)S(1)} %get-tuple-element.43), channel_id=1, source_target_pairs={{0,6},{2,14},{4,22},{6,30},{8,0},{10,8},{12,16},{14,24},{16,2},{18... | collective-permute-start | bytes 24584 | tf_op jit(solution)/shard_map/ppermute | solution.py:346
  61.6 0.0 collective-permute-done.15.refs_2_
  61.6 1.4 %collective-permute-done.16.refs_3_ = f32[16,128]{1,0:T(8,128)S(1)} collective-permute-done((f32[16,128]{1,0:T(8,128)S(1)}, f32[16,128]{1,0:T(8,128)S(1)}, u32[]{:S(2)}, u32[]{:S(2)}) %collective-permute-start.16) | collective-permute-done | bytes 8224 | tf_op jit(solution)/shard_map/ppermute | solution.py:346
  63.0 0.7 %shard_map.93 = f32[32,64]{1,0:T(8,128)} custom-call(f32[16,128]{1,0:T(8,128)S(1)} %collective-permute-done.13.refs_0_, f32[16,128]{1,0:T(8,128)S(1)} %collective-permute-done.14.refs_1_, f32[16,128]{1,0:T(8,128)S(1)} %collective-permute-done.15.refs_2_, f32[16,128]{1,0:T(8,128)S(1)} %collective-permute-done.16.refs_3_), custom_call_target="tpu_custom_call" | custom-call | flops 1000 | bytes 1048576 | tf_op jit(solution)/shard_map/pallas_call | solution.py:28
  63.6 0.0 collective-permute-done.8.refs_3_
  63.6 0.0 collective-permute-done.7.refs_2_
  63.6 0.0 collective-permute-done.6.refs_1_
  63.7 2.7 %shard_map.89 = bf16[1,64,1024]{2,1,0:T(8,128)(2,1)} custom-call(s32[1,3,1,8]{3,2,1,0:T(1,128)S(1)} %bitcast.11, s32[1,1]{1,0:T(1,128)S(6)} %copy.9.cnt_h, bf16[1,1,8,512,512]{4,3,2,1,0:T(8,128)(2,1)S(1)} %copy-done.1, bf16[64,1024]{1,0:T(8,128)(2,1)S(1)} %get-tuple-element.32.refs_0_, bf16[64,1024]{1,0:T(8,128)(2,1)S(1)} %collective-permute-done.6.refs_1_, ...), custom_call_target="tpu_custom_call" | custom-call | flops 1073741824 | bytes 1048576 | tf_op jit(solution)/shard_map/pallas_call | solution.py:28
  (10 shorter events, 0.0 us)
Async XLA Ops:
  0.6 22.4 %copy-start.7 = (s32[1,1,8,3]{2,1,3,0:T(1,128)S(1)}, s32[1,1,8,3]{2,1,3,0:T(1,128)}, u32[]{:S(2)}) copy-start(s32[1,1,8,3]{2,1,3,0:T(1,128)} %param.11) | copy-start | bytes 292
  0.6 0.9 %copy-start.2 = (bf16[1,1024,100]{1,2,0:T(8,128)(2,1)S(1)}, bf16[1,1024,100]{1,2,0:T(8,128)(2,1)}, u32[]{:S(2)}) copy-start(bf16[1,1024,100]{1,2,0:T(8,128)(2,1)} %param.7) | copy-start | bytes 614404
  1.6 0.8 %copy-start.4 = (bf16[64,256]{1,0:T(8,128)(2,1)S(1)}, bf16[64,256]{1,0:T(8,128)(2,1)}, u32[]{:S(2)}) copy-start(bf16[64,256]{1,0:T(8,128)(2,1)} %w_hid_h.1) | copy-start | bytes 98308
  2.3 0.7 %copy-start.5 = (bf16[100,64]{0,1:T(8,128)(2,1)S(1)}, bf16[100,64]{0,1:T(8,128)(2,1)}, u32[]{:S(2)}) copy-start(bf16[100,64]{0,1:T(8,128)(2,1)} %param.8) | copy-start | bytes 38404
  3.1 20.0 %copy-start.3 = (bf16[1,1024,64]{1,2,0:T(8,128)(2,1)S(1)}, bf16[1,1024,64]{1,2,0:T(8,128)(2,1)}, u32[]{:S(2)}) copy-start(bf16[1,1024,64]{1,2,0:T(8,128)(2,1)} %param.13) | copy-start | bytes 393220
  3.6 7.6 %collective-permute-start.2 = (bf16[32,1024]{1,0:T(8,128)(2,1)S(1)}, bf16[32,1024]{1,0:T(8,128)(2,1)S(1)}, u32[]{:S(2)}, u32[]{:S(2)}) collective-permute-start(bf16[32,1024]{1,0:T(8,128)(2,1)S(1)} %get-tuple-element.23.refs_0_), channel_id=1, source_target_pairs={{0,24},{8,0},{16,8},{24,16},{1,25},{9,1},{17,9},{25,17},{2,26},{10... | collective-permute-start | bytes 196616 | tf_op jit(solution)/shard_map/ppermute | solution.py:232
  8.7 6.5 %collective-permute-start.1 = (bf16[32,1024]{1,0:T(8,128)(2,1)S(1)}, bf16[32,1024]{1,0:T(8,128)(2,1)S(1)}, u32[]{:S(2)}, u32[]{:S(2)}) collective-permute-start(bf16[32,1024]{1,0:T(8,128)(2,1)S(1)} %get-tuple-element.23.refs_0_), channel_id=1, source_target_pairs={{0,16},{8,24},{16,0},{24,8},{1,17},{9,25},{17,1},{25,9},{2,18},{10... | collective-permute-start | bytes 196616 | tf_op jit(solution)/shard_map/ppermute | solution.py:232
  8.7 6.5 %collective-permute-start = (bf16[32,1024]{1,0:T(8,128)(2,1)S(1)}, bf16[32,1024]{1,0:T(8,128)(2,1)S(1)}, u32[]{:S(2)}, u32[]{:S(2)}) collective-permute-start(bf16[32,1024]{1,0:T(8,128)(2,1)S(1)} %get-tuple-element.23.refs_0_), channel_id=1, source_target_pairs={{0,8},{8,16},{16,24},{24,0},{1,9},{9,17},{17,25},{25,1},{2,10},{10... | collective-permute-start | bytes 196616 | tf_op jit(solution)/shard_map/ppermute | solution.py:232
  15.2 2.2 %copy-start = (bf16[1,1,8,512,512]{4,3,2,1,0:T(8,128)(2,1)S(1)}, bf16[1,1,8,512,512]{4,3,2,1,0:T(8,128)(2,1)}, u32[]{:S(2)}) copy-start(bf16[1,1,8,512,512]{4,3,2,1,0:T(8,128)(2,1)} %blocks.1) | copy-start | bytes 12582916
  17.4 0.7 %copy-start.6 = (s32[1,1,8,3]{2,1,3,0:T(1,128)S(1)}, s32[1,1,8,3]{2,1,3,0:T(1,128)}, u32[]{:S(2)}) copy-start(s32[1,1,8,3]{2,1,3,0:T(1,128)} %param.11) | copy-start | bytes 292
  20.0 8.8 %collective-permute-start.3 = (bf16[48,1024]{1,0:T(8,128)(2,1)S(1)}, bf16[48,1024]{1,0:T(8,128)(2,1)S(1)}, u32[]{:S(2)}, u32[]{:S(2)}) collective-permute-start(bf16[48,1024]{1,0:T(8,128)(2,1)S(1)} %get-tuple-element.29), channel_id=1, source_target_pairs={{0,2},{2,4},{4,6},{6,0},{1,3},{3,5},{5,7},{7,1},{8,10},{10,12},{12... | collective-permute-start | bytes 294920 | tf_op jit(solution)/shard_map/ppermute | solution.py:232
  20.1 10.9 %collective-permute-start.4 = (bf16[48,1024]{1,0:T(8,128)(2,1)S(1)}, bf16[48,1024]{1,0:T(8,128)(2,1)S(1)}, u32[]{:S(2)}, u32[]{:S(2)}) collective-permute-start(bf16[48,1024]{1,0:T(8,128)(2,1)S(1)} %get-tuple-element.30), channel_id=1, source_target_pairs={{0,4},{2,6},{4,0},{6,2},{1,5},{3,7},{5,1},{7,3},{8,12},{10,14},{12... | collective-permute-start | bytes 294920 | tf_op jit(solution)/shard_map/ppermute | solution.py:232
  21.7 9.4 %collective-permute-start.5 = (bf16[48,1024]{1,0:T(8,128)(2,1)S(1)}, bf16[48,1024]{1,0:T(8,128)(2,1)S(1)}, u32[]{:S(2)}, u32[]{:S(2)}) collective-permute-start(bf16[48,1024]{1,0:T(8,128)(2,1)S(1)} %get-tuple-element.31), channel_id=1, source_target_pairs={{0,6},{2,0},{4,2},{6,4},{1,7},{3,1},{5,3},{7,5},{8,14},{10,8},{12,... | collective-permute-start | bytes 294920 | tf_op jit(solution)/shard_map/ppermute | solution.py:232
  23.1 40.6 %copy-start.1 = (bf16[1,1,8,512,512]{4,3,2,1,0:T(8,128)(2,1)S(1)}, bf16[1,1,8,512,512]{4,3,2,1,0:T(8,128)(2,1)}, u32[]{:S(2)}) copy-start(bf16[1,1,8,512,512]{4,3,2,1,0:T(8,128)(2,1)} %blocks.1) | copy-start | bytes 12582916
  26.3 8.2 %collective-permute-start.9 = (bf16[64,1024]{1,0:T(8,128)(2,1)S(1)}, bf16[64,1024]{1,0:T(8,128)(2,1)S(1)}, u32[]{:S(2)}, u32[]{:S(2)}) collective-permute-start(bf16[64,1024]{1,0:T(8,128)(2,1)S(1)} %get-tuple-element.34), channel_id=1, source_target_pairs={{0,8},{8,16},{16,24},{24,0},{1,9},{9,17},{17,25},{25,1},{2,10},{10... | collective-permute-start | bytes 393224 | tf_op jit(solution)/shard_map/ppermute | solution.py:232
  26.5 17.1 %collective-permute-start.10 = (bf16[64,1024]{1,0:T(8,128)(2,1)S(1)}, bf16[64,1024]{1,0:T(8,128)(2,1)S(1)}, u32[]{:S(2)}, u32[]{:S(2)}) collective-permute-start(bf16[64,1024]{1,0:T(8,128)(2,1)S(1)} %get-tuple-element.35), channel_id=1, source_target_pairs={{0,16},{8,24},{16,0},{24,8},{1,17},{9,25},{17,1},{25,9},{2,18},{10... | collective-permute-start | bytes 393224 | tf_op jit(solution)/shard_map/ppermute | solution.py:232
  28.8 14.8 %collective-permute-start.11 = (bf16[64,1024]{1,0:T(8,128)(2,1)S(1)}, bf16[64,1024]{1,0:T(8,128)(2,1)S(1)}, u32[]{:S(2)}, u32[]{:S(2)}) collective-permute-start(bf16[64,1024]{1,0:T(8,128)(2,1)S(1)} %get-tuple-element.36), channel_id=1, source_target_pairs={{0,24},{8,0},{16,8},{24,16},{1,25},{9,1},{17,9},{25,17},{2,26},{10... | collective-permute-start | bytes 393224 | tf_op jit(solution)/shard_map/ppermute | solution.py:232
  32.1 31.5 %collective-permute-start.8 = (bf16[64,1024]{1,0:T(8,128)(2,1)S(1)}, bf16[64,1024]{1,0:T(8,128)(2,1)S(1)}, u32[]{:S(2)}, u32[]{:S(2)}) collective-permute-start(bf16[64,1024]{1,0:T(8,128)(2,1)S(1)} %get-tuple-element.32.refs_0_), channel_id=1, source_target_pairs={{0,24},{8,0},{16,8},{24,16},{1,25},{9,1},{17,9},{25,17},{2,26},{10... | collective-permute-start | bytes 393224 | tf_op jit(solution)/shard_map/ppermute | solution.py:232
  32.2 31.5 %collective-permute-start.7 = (bf16[64,1024]{1,0:T(8,128)(2,1)S(1)}, bf16[64,1024]{1,0:T(8,128)(2,1)S(1)}, u32[]{:S(2)}, u32[]{:S(2)}) collective-permute-start(bf16[64,1024]{1,0:T(8,128)(2,1)S(1)} %get-tuple-element.32.refs_0_), channel_id=1, source_target_pairs={{0,16},{8,24},{16,0},{24,8},{1,17},{9,25},{17,1},{25,9},{2,18},{10... | collective-permute-start | bytes 393224 | tf_op jit(solution)/shard_map/ppermute | solution.py:232
  34.5 29.1 %collective-permute-start.6 = (bf16[64,1024]{1,0:T(8,128)(2,1)S(1)}, bf16[64,1024]{1,0:T(8,128)(2,1)S(1)}, u32[]{:S(2)}, u32[]{:S(2)}) collective-permute-start(bf16[64,1024]{1,0:T(8,128)(2,1)S(1)} %get-tuple-element.32.refs_0_), channel_id=1, source_target_pairs={{0,8},{8,16},{16,24},{24,0},{1,9},{9,17},{17,25},{25,1},{2,10},{10... | collective-permute-start | bytes 393224 | tf_op jit(solution)/shard_map/ppermute | solution.py:232
  43.9 4.0 %collective-permute-start.12 = (f32[32,256]{1,0:T(8,128)S(1)}, f32[32,256]{1,0:T(8,128)S(1)}, u32[]{:S(2)}, u32[]{:S(2)}) collective-permute-start(f32[32,256]{1,0:T(8,128)S(1)} %get-tuple-element.39), channel_id=1, source_target_pairs={{0,1},{1,0},{2,3},{3,2},{4,5},{5,4},{6,7},{7,6},{8,9},{9,8},{10,11... | collective-permute-start | bytes 98312 | tf_op jit(solution)/shard_map/ppermute | solution.py:232
  47.9 4.9 %collective-permute-start.13 = (f32[16,128]{1,0:T(8,128)S(1)}, f32[16,128]{1,0:T(8,128)S(1)}, u32[]{:S(2)}, u32[]{:S(2)}) collective-permute-start(f32[16,128]{1,0:T(8,128)S(1)} %get-tuple-element.40), channel_id=1, source_target_pairs={{0,0},{2,8},{4,16},{6,24},{8,2},{10,10},{12,18},{14,26},{16,4},{18... | collective-permute-start | bytes 24584 | tf_op jit(solution)/shard_map/ppermute | solution.py:346
  48.6 8.6 %collective-permute-start.14 = (f32[16,128]{1,0:T(8,128)S(1)}, f32[16,128]{1,0:T(8,128)S(1)}, u32[]{:S(2)}, u32[]{:S(2)}) collective-permute-start(f32[16,128]{1,0:T(8,128)S(1)} %get-tuple-element.41), channel_id=1, source_target_pairs={{0,2},{2,10},{4,18},{6,26},{8,4},{10,12},{12,20},{14,28},{16,6},{1... | collective-permute-start | bytes 24584 | tf_op jit(solution)/shard_map/ppermute | solution.py:346
  52.8 8.8 %collective-permute-start.15 = (f32[16,128]{1,0:T(8,128)S(1)}, f32[16,128]{1,0:T(8,128)S(1)}, u32[]{:S(2)}, u32[]{:S(2)}) collective-permute-start(f32[16,128]{1,0:T(8,128)S(1)} %get-tuple-element.42), channel_id=1, source_target_pairs={{0,4},{2,12},{4,20},{6,28},{8,6},{10,14},{12,22},{14,30},{16,0},{1... | collective-permute-start | bytes 24584 | tf_op jit(solution)/shard_map/ppermute | solution.py:346
  57.2 5.8 %collective-permute-start.16 = (f32[16,128]{1,0:T(8,128)S(1)}, f32[16,128]{1,0:T(8,128)S(1)}, u32[]{:S(2)}, u32[]{:S(2)}) collective-permute-start(f32[16,128]{1,0:T(8,128)S(1)} %get-tuple-element.43), channel_id=1, source_target_pairs={{0,6},{2,14},{4,22},{6,30},{8,0},{10,8},{12,16},{14,24},{16,2},{18... | collective-permute-start | bytes 24584 | tf_op jit(solution)/shard_map/ppermute | solution.py:346

commit v2 on v1

v2 whole, which is shorter than its diff:
```python
import functools
import math

import jax
import jax.numpy as jnp
from jax import lax
from jax.experimental import pallas as pl
from jax.experimental.pallas import tpu as pltpu
from jax.sharding import PartitionSpec as P


BF = jnp.bfloat16
F32 = jnp.float32
VM = pl.BlockSpec(memory_space=pltpu.VMEM)
SM = pl.BlockSpec(memory_space=pltpu.SMEM)
HB = pl.BlockSpec(memory_space=pltpu.HBM)
LANES = 128
LIM = 24 << 20
PICK_LIM = 50 << 20
ROWS = 16


def dot(a, b):
    return jnp.dot(a, b, preferred_element_type=F32)


def call(kernel, ins, specs, outs, scratch=(), flops=0, limit=24 << 20, spaces=None):
    return pl.pallas_call(
        kernel,
        out_shape=outs,
        in_specs=specs,
        out_specs=spaces or jax.tree.map(lambda _: VM, outs),
        scratch_shapes=list(scratch),
        compiler_params=pltpu.CompilerParams(vmem_limit_bytes=limit),
        cost_estimate=pl.CostEstimate(flops=flops, bytes_accessed=1 << 20, transcendentals=0),
    )(*ins)


def ndot(a, b):
    return lax.dot_general(a, b, (((1,), (1,)), ((), ())), preferred_element_type=F32)


def onehot(mask):
    return mask.astype(F32).astype(BF)


def pick_kernel(feats, _, xp, *, per, lane):
    c = lax.axis_index("col")
    n_feat = feats.shape[1]
    row = lax.broadcasted_iota(jnp.int32, (lane, n_feat), 0)
    col = lax.broadcasted_iota(jnp.int32, (lane, n_feat), 1)
    mine = onehot((row < per) & (col == c * per + row))
    xp[...] = dot(mine, feats[0]).astype(BF)


def pack_kernel(w_in, w_hid, *refs, n_col, per, lane):
    wps = refs[:n_col]
    h_abs = refs[n_col]
    c = lax.axis_index("col")
    width, n_feat = w_in.shape
    frow = lax.broadcasted_iota(jnp.int32, (n_feat, LANES), 0)
    fcol = lax.broadcasted_iota(jnp.int32, (n_feat, LANES), 1)
    inner = lax.rem(fcol, lane)
    every = onehot((inner < per) & (frow == (fcol // lane) * per + inner))
    spread = dot(w_in[...], every).astype(BF)
    turned = w_hid[...].astype(F32).T.astype(BF)
    for t in range(n_col):
        h_abs[t] = turned[t * width : (t + 1) * width, :]
    for t in range(n_col):
        part = h_abs[c ^ t]
        wps[t][...] = jnp.zeros(wps[t].shape, BF)
        for m in range(width // ROWS):
            rows = slice(m * ROWS, (m + 1) * ROWS)
            wps[t][:, 2 * m * LANES : (2 * m + 1) * LANES] = spread[rows, :]
            wps[t][:, (2 * m + 1) * LANES : (2 * m + 1) * LANES + width] = part[rows, :]


def spread_kernel(lst_h, cnt, cot, held, tab, *refs, n_dom, slots, clus):
    outs = refs[:n_dom]
    lst, acc, sem = refs[n_dom:]
    copy = pltpu.make_async_copy(lst_h, lst, sem)
    copy.start()
    p = lax.axis_index("dom")
    cl = acc.shape[0] // n_dom
    acc[...] = jnp.zeros(acc.shape, F32)
    copy.wait()
    for m in range(3):
        for k in range(slots):
            tab[0, m * slots + k] = lst[0, m, 0, k]
    tab[0, 3 * slots] = cnt[0, 0]
    for k in range(slots):
        i = jnp.clip(tab[0, k], 0, cl - 1)
        at = (tab[0, slots + k] ^ p) * cl + tab[0, 2 * slots + k]
        at = jnp.clip(at, 0, n_dom * cl - 1)
        left = cot[0, :, pl.ds(pl.multiple_of(i * clus, LANES), clus)]
        left = jnp.where(k < tab[0, 3 * slots], left, jnp.zeros_like(left))
        acc[at] += dot(left, held[0, 0, k])
    for s in range(n_dom):
        for j in range(cl):
            outs[s][:, j * clus : (j + 1) * clus] = acc[s * cl + j].astype(outs[s].dtype)


def fold(tab, held, src, acc, n_dom, slots):
    cl = acc.shape[0]
    p = lax.axis_index("dom")
    acc[...] = jnp.zeros(acc.shape, F32)
    for k in range(slots):
        i = jnp.clip(tab[0, k], 0, cl - 1)
        at = (tab[0, slots + k] ^ p) * cl + tab[0, 2 * slots + k]
        left = src[jnp.clip(at, 0, n_dom * cl - 1)]
        left = jnp.where(k < tab[0, 3 * slots], left, jnp.zeros_like(left))
        acc[i] += ndot(left, held[0, 0, k])


def first_kernel(tab, held, *refs, n_dom, n_col, slots, clus, cl, lane):
    xs = refs[:n_dom]
    wps = refs[n_dom : n_dom + n_col]
    outs = refs[n_dom + n_col : n_dom + 2 * n_col]
    src, acc = refs[n_dom + 2 * n_col :]

    for s in range(n_dom):
        for j in range(cl):
            src[s * cl + j] = xs[s][:, j * clus : (j + 1) * clus]
    for t in range(n_col):
        outs[t][lane:, :] = wps[t][...]
    fold(tab, held, src, acc, n_dom, slots)
    for i in range(cl):
        part = acc[i].astype(BF)
        for t in range(n_col):
            outs[t][:lane, i * clus : (i + 1) * clus] = part


def gelu(v):
    return 0.5 * v * (1.0 + jnp.tanh(math.sqrt(2.0 / math.pi) * (v + 0.044715 * v * v * v)))


def hidden_kernel(*refs, n_col, lane, width):
    pays = refs[:n_col]
    h1, zp, ax, w1, w2 = refs[n_col:]
    c = lax.axis_index("col")
    for t in range(n_col):
        frm = c ^ t
        ax[frm] = pays[t][:lane, :]
        for m in range(width // ROWS):
            rows = slice(m * ROWS, (m + 1) * ROWS)
            w1[frm, rows, :] = pays[t][lane:, 2 * m * LANES : (2 * m + 1) * LANES]
            w2[frm, rows, :] = pays[t][lane:, (2 * m + 1) * LANES : (2 * m + 1) * LANES + width]
    left = w1[...].reshape(n_col * width, LANES)
    out = jnp.concatenate([w2[t] for t in range(n_col)], axis=1)
    nodes = h1.shape[1]
    right = ax[...].reshape(n_col * lane, nodes)
    step = nodes // 4
    for m in range(4):
        cols = slice(m * step, (m + 1) * step)
        h = gelu(dot(left, right[:, cols])).astype(BF)
        h1[:, cols] = h
        zp[:, cols] = dot(out, h).astype(BF)


def grad_kernel(*refs, n_dom, n_rep, wj):
    ys = refs[:n_dom]
    h1 = refs[n_dom]
    outs = refs[n_dom + 1 : -1]
    store = refs[-1]
    r = lax.axis_index("rep")
    total = ys[0][...]
    for y in ys[1:]:
        total = total + y[...].astype(F32)
    g = ndot(total.astype(BF), h1[...])
    for b in range(n_rep):
        store[b] = g[b * wj : (b + 1) * wj, :]
    for b in range(n_rep):
        outs[b][...] = store[r ^ b]


def pieces_kernel(*refs, n_col, n_rep, width, packs):
    parts = refs[:n_rep]
    outs = refs[n_rep:-1]
    store = refs[-1]
    d = lax.axis_index("dom")
    g = parts[0][...]
    for part in parts[1:]:
        g = g + part[...]
    rows = g.shape[0] // packs
    for t in range(n_col):
        for m in range(packs):
            store[t, :, m * width : (m + 1) * width] = g[m * rows : (m + 1) * rows, t * width : (t + 1) * width]
    for a in range(n_col):
        outs[a][...] = store[d ^ a]


def second_kernel(tab, held, *refs, n_dom, slots, clus, cl):
    zs = refs[:n_dom]
    out, src, acc = refs[n_dom:]
    for s in range(n_dom):
        for j in range(cl):
            src[s * cl + j] = zs[s][:, j * clus : (j + 1) * clus]
    fold(tab, held, src, acc, n_dom, slots)
    for i in range(cl):
        out[0, :, i * clus : (i + 1) * clus] = acc[i].astype(BF)


def sum_kernel(*refs, packs, width):
    pieces = refs[:-1]
    out = refs[-1]
    total = pieces[0][...]
    for piece in pieces[1:]:
        total = total + piece[...]
    rows = total.shape[0]
    for m in range(packs):
        out[m * rows : (m + 1) * rows, :] = total[:, m * width : (m + 1) * width]


def shifted(x, axis, size, s):
    return lax.ppermute(x, axis, [(i, i ^ s) for i in range(size)])


def partners(x, axis, size):
    parts = x if isinstance(x, (list, tuple)) else [x] * size
    return [parts[0]] + [shifted(parts[s], axis, size, s) for s in range(1, size)]


def body(features, w_in, w_hidden, blocks, block_list, block_count, cotangent):
    n_dom, n_col, n_rep = lax.axis_size("dom"), lax.axis_size("col"), lax.axis_size("rep")
    features = jnp.swapaxes(features, 1, 2)
    cotangent = jnp.swapaxes(cotangent, 1, 2)
    w_in = w_in.T
    block_list = jnp.transpose(block_list, (0, 3, 1, 2))
    n_feat, nodes = features.shape[1:]
    slots, clus = blocks.shape[2], blocks.shape[3]
    cl = nodes // clus
    width = w_in.shape[0]
    hid = width * n_col
    per = -(-n_feat // n_col)
    lane = LANES // n_col
    wj = hid // (n_dom * n_rep)
    assert n_dom == n_col and n_dom & (n_dom - 1) == 0 and n_rep & (n_rep - 1) == 0
    assert wj * n_rep == width and width % ROWS == 0
    assert per <= lane and lane % ROWS == 0 and width <= LANES and 2 * LANES * (width // ROWS) <= nodes
    packs = LANES // width if wj % (8 * (LANES // width)) == 0 else 1
    sds = jax.ShapeDtypeStruct
    block_flops = 2 * slots * clus * clus

    xp = call(
        functools.partial(pick_kernel, per=per, lane=lane),
        (features, blocks),
        [VM, HB],
        sds((lane, nodes), BF),
        flops=2 * nodes * n_feat * LANES,
        limit=PICK_LIM,
    )
    xs = partners(xp, "dom", n_dom)
    tab, *ys = call(
        functools.partial(spread_kernel, n_dom=n_dom, slots=slots, clus=clus),
        (block_list, block_count, cotangent, blocks),
        [HB, VM, VM, VM],
        [sds((1, LANES), jnp.int32), sds((width, nodes), F32)] + [sds((width, nodes), BF)] * (n_dom - 1),
        [
            pltpu.SMEM(block_list.shape, jnp.int32),
            pltpu.VMEM((n_dom * cl, width, clus), F32),
            pltpu.SemaphoreType.DMA,
        ],
        flops=block_flops * 256,
        limit=LIM,
        spaces=[SM] + [VM] * n_dom,
    )
    wps = call(
        functools.partial(pack_kernel, n_col=n_col, per=per, lane=lane),
        (w_in, w_hidden),
        [VM, VM],
        [sds((ROWS, nodes), BF)] * n_col,
        [pltpu.VMEM((n_col, width, width), BF)],
        flops=1000,
    )

    def fold_scratch(wide):
        return [pltpu.VMEM((n_dom * cl, wide, clus), BF), pltpu.VMEM((cl, wide, clus), F32)]

    pays = call(
        functools.partial(first_kernel, n_dom=n_dom, n_col=n_col, slots=slots, clus=clus, cl=cl, lane=lane),
        (tab, blocks, *xs, *wps),
        [SM] + [VM] * (1 + n_dom + n_col),
        [sds((lane + ROWS, nodes), BF)] * n_col,
        fold_scratch(lane),
        flops=block_flops * 256,
        limit=LIM,
    )
    pays = partners(pays, "col", n_col)
    ys = partners(ys, "dom", n_dom)
    h1, zp = call(
        functools.partial(hidden_kernel, n_col=n_col, lane=lane, width=width),
        pays,
        [VM] * n_col,
        [sds((hid, nodes), BF), sds((width, nodes), BF)],
        [
            pltpu.VMEM((n_col, lane, nodes), BF),
            pltpu.VMEM((n_col, width, LANES), BF),
            pltpu.VMEM((n_col, width, width), BF),
        ],
        flops=2 * nodes * n_col * LANES * hid * 4,
    )
    zs = partners(zp, "dom", n_dom)
    halves = call(
        functools.partial(grad_kernel, n_dom=n_dom, n_rep=n_rep, wj=wj),
        (*ys, h1),
        [VM] * (n_dom + 1),
        [sds((wj, hid), F32)] * n_rep,
        [pltpu.VMEM((n_rep, wj, hid), F32)],
        flops=2 * nodes * hid * width * 4,
    )
    halves = partners(halves, "rep", n_rep)
    pieces = call(
        functools.partial(pieces_kernel, n_col=n_col, n_rep=n_rep, width=width, packs=packs),
        halves,
        [VM] * n_rep,
        [sds((wj // packs, packs * width), F32)] * n_col,
        [pltpu.VMEM((n_col, wj // packs, packs * width), F32)],
        flops=1000,
    )
    grads = []
    for a in range(n_col):
        pairs = []
        for d in range(n_dom):
            for c in range(n_col):
                pairs.append((d * n_col + c, c * n_col + (d ^ a)))
        grads.append(lax.ppermute(pieces[a], ("dom", "col"), pairs))
    out = call(
        functools.partial(second_kernel, n_dom=n_dom, slots=slots, clus=clus, cl=cl),
        (tab, blocks, *zs),
        [SM] + [VM] * (1 + n_dom),
        sds((1, width, nodes), BF),
        fold_scratch(width),
        flops=block_flops * 256,
        limit=LIM,
    )
    grad = call(
        functools.partial(sum_kernel, packs=packs, width=width),
        grads,
        [VM] * n_col,
        sds((wj, width), F32),
        flops=1000,
    )
    return jnp.swapaxes(out, 1, 2), grad.T


def solution(mesh):
    placed = (
        P("rep", "dom", None),
        P(None, "col"),
        P("col", None),
        P("rep", "dom", None, None, None),
        P("rep", "dom", None, None),
        P("rep", "dom"),
        P("rep", "dom", "col"),
    )

    return jax.shard_map(
        body,
        mesh=mesh,
        in_specs=placed,
        out_specs=(P("rep", "dom", "col"), P("col", ("dom", "rep"))),
        check_vma=False,
    )
```

time: 66.6 us -> 59.2 us (0.89)
  the two profiles are of different devices: /device:TPU:0 before, /device:TPU:4 now
where the time goes in v2:
time: 59.2 us; the launch traced here: 59.1 us
  starting transfers between devices  24.2 us (41%)
  waiting for transfers between devices  23.7 us (40%)
  Pallas kernels  8.68 us (15%)
  between operations  1.43 us (2%)
  local copies, waits for them, and re-layouts  1.09 us (2%)
    ppermute x13, starting transfers between devices, shifted(): return lax.ppermute(x, axis, [(i, i ^ s) for i in range(size)])  16.8 us
    ppermute x13, waiting for transfers between devices, shifted(): return lax.ppermute(x, axis, [(i, i ^ s) for i in range(size)])  14.3 us
    ppermute x4, waiting for transfers between devices, body(): grads.append(lax.ppermute(pieces[a], ('dom', 'col'), pairs))  9.34 us
    pallas_call x9, Pallas kernels, call(): pl.pallas_call(kernel, out_shape=outs, in_specs=specs, out_specs=spaces o...  8.68 us
    ppermute x4, starting transfers between devices, body(): grads.append(lax.ppermute(pieces[a], ('dom', 'col'), pairs))  7.42 us
  transfers between devices with their start and end apart: 17, of which 6 were waited for; matrix products, arithmetic and copies ran while one was open for 0% of the time, Pallas kernels for 7%

profile of v2, /device:TPU:4, one launch (start us, length us, event | category | flops | bytes accessed | tf_op | source)
XLA Modules:
  0.0 59.1 jit_solution(7767027478511458927)
XLA Ops:
  0.7 1.1 %copy-done.1 = bf16[1,1024,100]{1,2,0:T(8,128)(2,1)S(1)} copy-done((bf16[1,1024,100]{1,2,0:T(8,128)(2,1)S(1)}, bf16[1,1024,100]{1,2,0:T(8,128)(2,1)}, u32[]{:S(2)}) %copy-start.1) | copy-done | bytes 204824
  1.7 0.1 shard_map.87.refs_0_
  1.9 3.7 %collective-permute-start.2 = (bf16[32,1024]{1,0:T(8,128)(2,1)S(1)}, bf16[32,1024]{1,0:T(8,128)(2,1)S(1)}, u32[]{:S(2)}, u32[]{:S(2)}) collective-permute-start(bf16[32,1024]{1,0:T(8,128)(2,1)S(1)} %shard_map.87.refs_0_), channel_id=1, source_target_pairs={{0,24},{8,16},{16,8},{24,0},{1,25},{9,17},{17,9},{25,1},{2,26},{10... | collective-permute-start | bytes 196616 | tf_op jit(solution)/shard_map/ppermute | solution.py:215
  5.6 0.0 collective-permute-start.1
  5.6 0.8 %collective-permute-start = (bf16[32,1024]{1,0:T(8,128)(2,1)S(1)}, bf16[32,1024]{1,0:T(8,128)(2,1)S(1)}, u32[]{:S(2)}, u32[]{:S(2)}) collective-permute-start(bf16[32,1024]{1,0:T(8,128)(2,1)S(1)} %shard_map.87.refs_0_), channel_id=1, source_target_pairs={{0,8},{8,0},{16,24},{24,16},{1,9},{9,1},{17,25},{25,17},{2,10},{10... | collective-permute-start | bytes 196616 | tf_op jit(solution)/shard_map/ppermute | solution.py:215
  7.0 0.0 copy-done.3
  7.0 0.0 copy-done.4
  7.0 0.1 shard_map.88
  7.2 0.0 copy-done
  7.2 0.0 copy-done.2
  7.2 1.8 %shard_map.86 = (s32[1,128]{1,0:T(1,128)S(1)}, f32[64,1024]{1,0:T(8,128)S(1)}, bf16[64,1024]{1,0:T(8,128)(2,1)S(1)}, bf16[64,1024]{1,0:T(8,128)(2,1)S(1)}, bf16[64,1024]{1,0:T(8,128)(2,1)S(1)}) custom-call(s32[1,3,1,8]{3,2,1,0:T(1,128)S(1)} %bitcast.9, s32[1,1]{1,0:T(1,128)S(6)} %copy.9.cnt, bf16[1,64,1024]{2,1,0:T(8,128)(2,1)S(1)} %bitcast.7, ...), custom_call_target="tpu_custom_call" | custom-call | flops 1073741824 | bytes 1048576 | tf_op jit(solution)/shard_map/pallas_call | solution.py:28
  9.0 0.0 collective-permute-done.2.refs_3_
  9.0 2.1 %collective-permute-done.1.refs_2_ = bf16[32,1024]{1,0:T(8,128)(2,1)S(1)} collective-permute-done((bf16[32,1024]{1,0:T(8,128)(2,1)S(1)}, bf16[32,1024]{1,0:T(8,128)(2,1)S(1)}, u32[]{:S(2)}, u32[]{:S(2)}) %collective-permute-start.1) | collective-permute-done | bytes 65568 | tf_op jit(solution)/shard_map/ppermute | solution.py:215
  11.2 0.0 collective-permute-done.refs_1_
  11.2 1.9 %shard_map.89 = (bf16[48,1024]{1,0:T(8,128)(2,1)S(1)}, bf16[48,1024]{1,0:T(8,128)(2,1)S(1)}, bf16[48,1024]{1,0:T(8,128)(2,1)S(1)}, bf16[48,1024]{1,0:T(8,128)(2,1)S(1)}) custom-call(s32[1,128]{1,0:T(1,128)S(1)} %get-tuple-element.23.tab, bf16[1,1,8,512,512]{4,3,2,1,0:T(8,128)(2,1)S(1)} %copy-done, bf16[32,1024]{1,0:T(8,128)(2,1)S(1)} %shard_map.87.refs_0_, ...), custom_call_target="tpu_custom_call" | custom-call | flops 1073741824 | bytes 1048576 | tf_op jit(solution)/shard_map/pallas_call | solution.py:28
  13.1 0.1 collective-permute-start.3
  13.1 0.6 collective-permute-start.4
  13.7 1.3 %collective-permute-start.5 = (bf16[48,1024]{1,0:T(8,128)(2,1)S(1)}, bf16[48,1024]{1,0:T(8,128)(2,1)S(1)}, u32[]{:S(2)}, u32[]{:S(2)}) collective-permute-start(bf16[48,1024]{1,0:T(8,128)(2,1)S(1)} %get-tuple-element.31), channel_id=1, source_target_pairs={{0,6},{2,4},{4,2},{6,0},{1,7},{3,5},{5,3},{7,1},{8,14},{10,12},{12... | collective-permute-start | bytes 294920 | tf_op jit(solution)/shard_map/ppermute | solution.py:215
  15.0 1.1 %collective-permute-start.9 = (bf16[64,1024]{1,0:T(8,128)(2,1)S(1)}, bf16[64,1024]{1,0:T(8,128)(2,1)S(1)}, u32[]{:S(2)}, u32[]{:S(2)}) collective-permute-start(bf16[64,1024]{1,0:T(8,128)(2,1)S(1)} %get-tuple-element.34), channel_id=1, source_target_pairs={{0,8},{8,0},{16,24},{24,16},{1,9},{9,1},{17,25},{25,17},{2,10},{10... | collective-permute-start | bytes 393224 | tf_op jit(solution)/shard_map/ppermute | solution.py:215
  16.1 2.2 %collective-permute-start.10 = (bf16[64,1024]{1,0:T(8,128)(2,1)S(1)}, bf16[64,1024]{1,0:T(8,128)(2,1)S(1)}, u32[]{:S(2)}, u32[]{:S(2)}) collective-permute-start(bf16[64,1024]{1,0:T(8,128)(2,1)S(1)} %get-tuple-element.35), channel_id=1, source_target_pairs={{0,16},{8,24},{16,0},{24,8},{1,17},{9,25},{17,1},{25,9},{2,18},{10... | collective-permute-start | bytes 393224 | tf_op jit(solution)/shard_map/ppermute | solution.py:215
  18.3 0.0 collective-permute-done.3.refs_1_
  18.3 1.1 %collective-permute-start.11 = (bf16[64,1024]{1,0:T(8,128)(2,1)S(1)}, bf16[64,1024]{1,0:T(8,128)(2,1)S(1)}, u32[]{:S(2)}, u32[]{:S(2)}) collective-permute-start(bf16[64,1024]{1,0:T(8,128)(2,1)S(1)} %get-tuple-element.36), channel_id=1, source_target_pairs={{0,24},{8,16},{16,8},{24,0},{1,25},{9,17},{17,9},{25,1},{2,26},{10... | collective-permute-start | bytes 393224 | tf_op jit(solution)/shard_map/ppermute | solution.py:215
  19.4 0.0 collective-permute-done.4.refs_2_
  19.4 0.5 collective-permute-done.5.refs_3_
  19.9 1.1 %shard_map.90 = (bf16[256,1024]{1,0:T(8,128)(2,1)S(1)}, bf16[64,1024]{1,0:T(8,128)(2,1)S(1)}) custom-call(bf16[48,1024]{1,0:T(8,128)(2,1)S(1)} %get-tuple-element.28.refs_0_, bf16[48,1024]{1,0:T(8,128)(2,1)S(1)} %collective-permute-done.3.refs_1_, bf16[48,1024]{1,0:T(8,128)(2,1)S(1)} %collective-permute-done.4.refs_2_, ...), custom_call_target="tpu_custom_call" | custom-call | flops 1073741824 | bytes 1048576 | tf_op jit(solution)/shard_map/pallas_call | solution.py:28
  21.0 2.8 %collective-permute-start.8 = (bf16[64,1024]{1,0:T(8,128)(2,1)S(1)}, bf16[64,1024]{1,0:T(8,128)(2,1)S(1)}, u32[]{:S(2)}, u32[]{:S(2)}) collective-permute-start(bf16[64,1024]{1,0:T(8,128)(2,1)S(1)} %get-tuple-element.32.refs_0_), channel_id=1, source_target_pairs={{0,24},{8,16},{16,8},{24,0},{1,25},{9,17},{17,9},{25,1},{2,26},{10... | collective-permute-start | bytes 393224 | tf_op jit(solution)/shard_map/ppermute | solution.py:215
  23.8 0.0 collective-permute-start.7
  23.8 0.0 collective-permute-done.9.refs_1_
  23.8 1.7 %collective-permute-start.6 = (bf16[64,1024]{1,0:T(8,128)(2,1)S(1)}, bf16[64,1024]{1,0:T(8,128)(2,1)S(1)}, u32[]{:S(2)}, u32[]{:S(2)}) collective-permute-start(bf16[64,1024]{1,0:T(8,128)(2,1)S(1)} %get-tuple-element.32.refs_0_), channel_id=1, source_target_pairs={{0,8},{8,0},{16,24},{24,16},{1,9},{9,1},{17,25},{25,17},{2,10},{10... | collective-permute-start | bytes 393224 | tf_op jit(solution)/shard_map/ppermute | solution.py:215
  25.4 9.2 %collective-permute-done.10.refs_2_ = bf16[64,1024]{1,0:T(8,128)(2,1)S(1)} collective-permute-done((bf16[64,1024]{1,0:T(8,128)(2,1)S(1)}, bf16[64,1024]{1,0:T(8,128)(2,1)S(1)}, u32[]{:S(2)}, u32[]{:S(2)}) %collective-permute-start.10) | collective-permute-done | bytes 131104 | tf_op jit(solution)/shard_map/ppermute | solution.py:215
  34.7 0.0 collective-permute-done.11.refs_3_
  34.7 0.3 shard_map.92
  35.0 1.6 %collective-permute-start.12 = (f32[32,256]{1,0:T(8,128)S(1)}, f32[32,256]{1,0:T(8,128)S(1)}, u32[]{:S(2)}, u32[]{:S(2)}) collective-permute-start(f32[32,256]{1,0:T(8,128)S(1)} %get-tuple-element.39), channel_id=1, source_target_pairs={{0,1},{1,0},{2,3},{3,2},{4,5},{5,4},{6,7},{7,6},{8,9},{9,8},{10,11... | collective-permute-start | bytes 98312 | tf_op jit(solution)/shard_map/ppermute | solution.py:215
  36.5 2.4 %collective-permute-done.12.refs_1_ = f32[32,256]{1,0:T(8,128)S(1)} collective-permute-done((f32[32,256]{1,0:T(8,128)S(1)}, f32[32,256]{1,0:T(8,128)S(1)}, u32[]{:S(2)}, u32[]{:S(2)}) %collective-permute-start.12) | collective-permute-done | bytes 32800 | tf_op jit(solution)/shard_map/ppermute | solution.py:215
  38.9 0.1 shard_map.93
  39.0 5.7 %collective-permute-start.13 = (f32[16,128]{1,0:T(8,128)S(1)}, f32[16,128]{1,0:T(8,128)S(1)}, u32[]{:S(2)}, u32[]{:S(2)}) collective-permute-start(f32[16,128]{1,0:T(8,128)S(1)} %get-tuple-element.40), channel_id=1, source_target_pairs={{0,0},{2,8},{4,16},{6,24},{8,2},{10,10},{12,18},{14,26},{16,4},{18... | collective-permute-start | bytes 24584 | tf_op jit(solution)/shard_map/ppermute | solution.py:326
  44.8 1.7 %collective-permute-start.14 = (f32[16,128]{1,0:T(8,128)S(1)}, f32[16,128]{1,0:T(8,128)S(1)}, u32[]{:S(2)}, u32[]{:S(2)}) collective-permute-start(f32[16,128]{1,0:T(8,128)S(1)} %get-tuple-element.41), channel_id=1, source_target_pairs={{0,2},{2,10},{4,18},{6,26},{8,0},{10,8},{12,16},{14,24},{16,6},{18... | collective-permute-start | bytes 24584 | tf_op jit(solution)/shard_map/ppermute | solution.py:326
  46.4 0.0 collective-permute-done.13.refs_0_
  46.4 0.0 collective-permute-start.15
  46.5 4.8 %collective-permute-done.14.refs_1_ = f32[16,128]{1,0:T(8,128)S(1)} collective-permute-done((f32[16,128]{1,0:T(8,128)S(1)}, f32[16,128]{1,0:T(8,128)S(1)}, u32[]{:S(2)}, u32[]{:S(2)}) %collective-permute-start.14) | collective-permute-done | bytes 8224 | tf_op jit(solution)/shard_map/ppermute | solution.py:326
  51.2 0.0 collective-permute-start.16
  51.2 0.0 collective-permute-done.15.refs_2_
  51.2 4.5 %collective-permute-done.16.refs_3_ = f32[16,128]{1,0:T(8,128)S(1)} collective-permute-done((f32[16,128]{1,0:T(8,128)S(1)}, f32[16,128]{1,0:T(8,128)S(1)}, u32[]{:S(2)}, u32[]{:S(2)}) %collective-permute-start.16) | collective-permute-done | bytes 8224 | tf_op jit(solution)/shard_map/ppermute | solution.py:326
  55.8 0.7 %shard_map.94 = f32[32,64]{1,0:T(8,128)} custom-call(f32[16,128]{1,0:T(8,128)S(1)} %collective-permute-done.13.refs_0_, f32[16,128]{1,0:T(8,128)S(1)} %collective-permute-done.14.refs_1_, f32[16,128]{1,0:T(8,128)S(1)} %collective-permute-done.15.refs_2_, f32[16,128]{1,0:T(8,128)S(1)} %collective-permute-done.16.refs_3_), custom_call_target="tpu_custom_call" | custom-call | flops 1000 | bytes 1048576 | tf_op jit(solution)/shard_map/pallas_call | solution.py:28
  56.5 0.0 collective-permute-done.8.refs_3_
  56.5 0.0 collective-permute-done.7.refs_2_
  56.5 0.0 collective-permute-done.6.refs_1_
  56.5 2.6 %shard_map.91 = bf16[1,64,1024]{2,1,0:T(8,128)(2,1)} custom-call(s32[1,128]{1,0:T(1,128)S(1)} %get-tuple-element.23.tab, bf16[1,1,8,512,512]{4,3,2,1,0:T(8,128)(2,1)S(1)} %copy-done, bf16[64,1024]{1,0:T(8,128)(2,1)S(1)} %get-tuple-element.32.refs_0_, bf16[64,1024]{1,0:T(8,128)(2,1)S(1)} %collective-permute-done.6.refs_1_, ...), custom_call_target="tpu_custom_call" | custom-call | flops 1073741824 | bytes 1048576 | tf_op jit(solution)/shard_map/pallas_call | solution.py:28
  (7 shorter events, 0.0 us)
Async XLA Ops:
  0.6 6.5 %copy-start = (bf16[1,1,8,512,512]{4,3,2,1,0:T(8,128)(2,1)S(1)}, bf16[1,1,8,512,512]{4,3,2,1,0:T(8,128)(2,1)}, u32[]{:S(2)}) copy-start(bf16[1,1,8,512,512]{4,3,2,1,0:T(8,128)(2,1)} %held.5) | copy-start | bytes 12582916
  0.6 1.1 %copy-start.1 = (bf16[1,1024,100]{1,2,0:T(8,128)(2,1)S(1)}, bf16[1,1024,100]{1,2,0:T(8,128)(2,1)}, u32[]{:S(2)}) copy-start(bf16[1,1024,100]{1,2,0:T(8,128)(2,1)} %param.7) | copy-start | bytes 614404
  1.7 5.3 %copy-start.3 = (bf16[64,256]{1,0:T(8,128)(2,1)S(1)}, bf16[64,256]{1,0:T(8,128)(2,1)}, u32[]{:S(2)}) copy-start(bf16[64,256]{1,0:T(8,128)(2,1)} %w_hid.1) | copy-start | bytes 98308
  1.7 5.3 %copy-start.4 = (bf16[100,64]{0,1:T(8,128)(2,1)S(1)}, bf16[100,64]{0,1:T(8,128)(2,1)}, u32[]{:S(2)}) copy-start(bf16[100,64]{0,1:T(8,128)(2,1)} %param.8) | copy-start | bytes 38404
  1.7 5.4 %copy-start.2 = (bf16[1,1024,64]{1,2,0:T(8,128)(2,1)S(1)}, bf16[1,1024,64]{1,2,0:T(8,128)(2,1)}, u32[]{:S(2)}) copy-start(bf16[1,1024,64]{1,2,0:T(8,128)(2,1)} %param.13) | copy-start | bytes 393220
  1.7 5.5 %copy-start.5 = (s32[1,1,8,3]{2,1,3,0:T(1,128)S(1)}, s32[1,1,8,3]{2,1,3,0:T(1,128)}, u32[]{:S(2)}) copy-start(s32[1,1,8,3]{2,1,3,0:T(1,128)} %param.11) | copy-start | bytes 292
  1.9 7.1 %collective-permute-start.2 = (bf16[32,1024]{1,0:T(8,128)(2,1)S(1)}, bf16[32,1024]{1,0:T(8,128)(2,1)S(1)}, u32[]{:S(2)}, u32[]{:S(2)}) collective-permute-start(bf16[32,1024]{1,0:T(8,128)(2,1)S(1)} %shard_map.87.refs_0_), channel_id=1, source_target_pairs={{0,24},{8,16},{16,8},{24,0},{1,25},{9,17},{17,9},{25,1},{2,26},{10... | collective-permute-start | bytes 196616 | tf_op jit(solution)/shard_map/ppermute | solution.py:215
  5.6 5.6 %collective-permute-start.1 = (bf16[32,1024]{1,0:T(8,128)(2,1)S(1)}, bf16[32,1024]{1,0:T(8,128)(2,1)S(1)}, u32[]{:S(2)}, u32[]{:S(2)}) collective-permute-start(bf16[32,1024]{1,0:T(8,128)(2,1)S(1)} %shard_map.87.refs_0_), channel_id=1, source_target_pairs={{0,16},{8,24},{16,0},{24,8},{1,17},{9,25},{17,1},{25,9},{2,18},{10... | collective-permute-start | bytes 196616 | tf_op jit(solution)/shard_map/ppermute | solution.py:215
  5.6 5.6 %collective-permute-start = (bf16[32,1024]{1,0:T(8,128)(2,1)S(1)}, bf16[32,1024]{1,0:T(8,128)(2,1)S(1)}, u32[]{:S(2)}, u32[]{:S(2)}) collective-permute-start(bf16[32,1024]{1,0:T(8,128)(2,1)S(1)} %shard_map.87.refs_0_), channel_id=1, source_target_pairs={{0,8},{8,0},{16,24},{24,16},{1,9},{9,1},{17,25},{25,17},{2,10},{10... | collective-permute-start | bytes 196616 | tf_op jit(solution)/shard_map/ppermute | solution.py:215
  13.1 5.2 %collective-permute-start.3 = (bf16[48,1024]{1,0:T(8,128)(2,1)S(1)}, bf16[48,1024]{1,0:T(8,128)(2,1)S(1)}, u32[]{:S(2)}, u32[]{:S(2)}) collective-permute-start(bf16[48,1024]{1,0:T(8,128)(2,1)S(1)} %get-tuple-element.29), channel_id=1, source_target_pairs={{0,2},{2,0},{4,6},{6,4},{1,3},{3,1},{5,7},{7,5},{8,10},{10,8},{12,... | collective-permute-start | bytes 294920 | tf_op jit(solution)/shard_map/ppermute | solution.py:215
  13.1 6.2 %collective-permute-start.4 = (bf16[48,1024]{1,0:T(8,128)(2,1)S(1)}, bf16[48,1024]{1,0:T(8,128)(2,1)S(1)}, u32[]{:S(2)}, u32[]{:S(2)}) collective-permute-start(bf16[48,1024]{1,0:T(8,128)(2,1)S(1)} %get-tuple-element.30), channel_id=1, source_target_pairs={{0,4},{2,6},{4,0},{6,2},{1,5},{3,7},{5,1},{7,3},{8,12},{10,14},{12... | collective-permute-start | bytes 294920 | tf_op jit(solution)/shard_map/ppermute | solution.py:215
  13.7 6.2 %collective-permute-start.5 = (bf16[48,1024]{1,0:T(8,128)(2,1)S(1)}, bf16[48,1024]{1,0:T(8,128)(2,1)S(1)}, u32[]{:S(2)}, u32[]{:S(2)}) collective-permute-start(bf16[48,1024]{1,0:T(8,128)(2,1)S(1)} %get-tuple-element.31), channel_id=1, source_target_pairs={{0,6},{2,4},{4,2},{6,0},{1,7},{3,5},{5,3},{7,1},{8,14},{10,12},{12... | collective-permute-start | bytes 294920 | tf_op jit(solution)/shard_map/ppermute | solution.py:215
  15.0 8.8 %collective-permute-start.9 = (bf16[64,1024]{1,0:T(8,128)(2,1)S(1)}, bf16[64,1024]{1,0:T(8,128)(2,1)S(1)}, u32[]{:S(2)}, u32[]{:S(2)}) collective-permute-start(bf16[64,1024]{1,0:T(8,128)(2,1)S(1)} %get-tuple-element.34), channel_id=1, source_target_pairs={{0,8},{8,0},{16,24},{24,16},{1,9},{9,1},{17,25},{25,17},{2,10},{10... | collective-permute-start | bytes 393224 | tf_op jit(solution)/shard_map/ppermute | solution.py:215
  16.1 18.6 %collective-permute-start.10 = (bf16[64,1024]{1,0:T(8,128)(2,1)S(1)}, bf16[64,1024]{1,0:T(8,128)(2,1)S(1)}, u32[]{:S(2)}, u32[]{:S(2)}) collective-permute-start(bf16[64,1024]{1,0:T(8,128)(2,1)S(1)} %get-tuple-element.35), channel_id=1, source_target_pairs={{0,16},{8,24},{16,0},{24,8},{1,17},{9,25},{17,1},{25,9},{2,18},{10... | collective-permute-start | bytes 393224 | tf_op jit(solution)/shard_map/ppermute | solution.py:215
  18.3 16.4 %collective-permute-start.11 = (bf16[64,1024]{1,0:T(8,128)(2,1)S(1)}, bf16[64,1024]{1,0:T(8,128)(2,1)S(1)}, u32[]{:S(2)}, u32[]{:S(2)}) collective-permute-start(bf16[64,1024]{1,0:T(8,128)(2,1)S(1)} %get-tuple-element.36), channel_id=1, source_target_pairs={{0,24},{8,16},{16,8},{24,0},{1,25},{9,17},{17,9},{25,1},{2,26},{10... | collective-permute-start | bytes 393224 | tf_op jit(solution)/shard_map/ppermute | solution.py:215
  21.0 35.5 %collective-permute-start.8 = (bf16[64,1024]{1,0:T(8,128)(2,1)S(1)}, bf16[64,1024]{1,0:T(8,128)(2,1)S(1)}, u32[]{:S(2)}, u32[]{:S(2)}) collective-permute-start(bf16[64,1024]{1,0:T(8,128)(2,1)S(1)} %get-tuple-element.32.refs_0_), channel_id=1, source_target_pairs={{0,24},{8,16},{16,8},{24,0},{1,25},{9,17},{17,9},{25,1},{2,26},{10... | collective-permute-start | bytes 393224 | tf_op jit(solution)/shard_map/ppermute | solution.py:215
  23.8 32.7 %collective-permute-start.7 = (bf16[64,1024]{1,0:T(8,128)(2,1)S(1)}, bf16[64,1024]{1,0:T(8,128)(2,1)S(1)}, u32[]{:S(2)}, u32[]{:S(2)}) collective-permute-start(bf16[64,1024]{1,0:T(8,128)(2,1)S(1)} %get-tuple-element.32.refs_0_), channel_id=1, source_target_pairs={{0,16},{8,24},{16,0},{24,8},{1,17},{9,25},{17,1},{25,9},{2,18},{10... | collective-permute-start | bytes 393224 | tf_op jit(solution)/shard_map/ppermute | solution.py:215
  23.8 32.7 %collective-permute-start.6 = (bf16[64,1024]{1,0:T(8,128)(2,1)S(1)}, bf16[64,1024]{1,0:T(8,128)(2,1)S(1)}, u32[]{:S(2)}, u32[]{:S(2)}) collective-permute-start(bf16[64,1024]{1,0:T(8,128)(2,1)S(1)} %get-tuple-element.32.refs_0_), channel_id=1, source_target_pairs={{0,8},{8,0},{16,24},{24,16},{1,9},{9,1},{17,25},{25,17},{2,10},{10... | collective-permute-start | bytes 393224 | tf_op jit(solution)/shard_map/ppermute | solution.py:215
  35.0 4.0 %collective-permute-start.12 = (f32[32,256]{1,0:T(8,128)S(1)}, f32[32,256]{1,0:T(8,128)S(1)}, u32[]{:S(2)}, u32[]{:S(2)}) collective-permute-start(f32[32,256]{1,0:T(8,128)S(1)} %get-tuple-element.39), channel_id=1, source_target_pairs={{0,1},{1,0},{2,3},{3,2},{4,5},{5,4},{6,7},{7,6},{8,9},{9,8},{10,11... | collective-permute-start | bytes 98312 | tf_op jit(solution)/shard_map/ppermute | solution.py:215
  39.0 7.4 %collective-permute-start.13 = (f32[16,128]{1,0:T(8,128)S(1)}, f32[16,128]{1,0:T(8,128)S(1)}, u32[]{:S(2)}, u32[]{:S(2)}) collective-permute-start(f32[16,128]{1,0:T(8,128)S(1)} %get-tuple-element.40), channel_id=1, source_target_pairs={{0,0},{2,8},{4,16},{6,24},{8,2},{10,10},{12,18},{14,26},{16,4},{18... | collective-permute-start | bytes 24584 | tf_op jit(solution)/shard_map/ppermute | solution.py:326
  44.8 6.5 %collective-permute-start.14 = (f32[16,128]{1,0:T(8,128)S(1)}, f32[16,128]{1,0:T(8,128)S(1)}, u32[]{:S(2)}, u32[]{:S(2)}) collective-permute-start(f32[16,128]{1,0:T(8,128)S(1)} %get-tuple-element.41), channel_id=1, source_target_pairs={{0,2},{2,10},{4,18},{6,26},{8,0},{10,8},{12,16},{14,24},{16,6},{18... | collective-permute-start | bytes 24584 | tf_op jit(solution)/shard_map/ppermute | solution.py:326
  46.4 4.8 %collective-permute-start.15 = (f32[16,128]{1,0:T(8,128)S(1)}, f32[16,128]{1,0:T(8,128)S(1)}, u32[]{:S(2)}, u32[]{:S(2)}) collective-permute-start(f32[16,128]{1,0:T(8,128)S(1)} %get-tuple-element.42), channel_id=1, source_target_pairs={{0,4},{2,12},{4,20},{6,28},{8,6},{10,14},{12,22},{14,30},{16,0},{1... | collective-permute-start | bytes 24584 | tf_op jit(solution)/shard_map/ppermute | solution.py:326
  51.2 4.5 %collective-permute-start.16 = (f32[16,128]{1,0:T(8,128)S(1)}, f32[16,128]{1,0:T(8,128)S(1)}, u32[]{:S(2)}, u32[]{:S(2)}) collective-permute-start(f32[16,128]{1,0:T(8,128)S(1)} %get-tuple-element.43), channel_id=1, source_target_pairs={{0,6},{2,14},{4,22},{6,30},{8,4},{10,12},{12,20},{14,28},{16,2},{1... | collective-permute-start | bytes 24584 | tf_op jit(solution)/shard_map/ppermute | solution.py:326
